TPU v7x, 256 devices: a 8x8x2 block of a 8x8x16 slice. The times are simulated.
256 devices in a mesh: groups: 2 (over z), ref: 128 (over x, y, core).
Axes of the slice: x: 8, y: 8, z: 2, core: 2. Of those that a mesh axis runs over, the one named last changes fastest.
The devices are a block of a 8x8x16 slice.
Arguments:
- long_series: bfloat16 [1048576], P(('groups', 'ref')), parts along dimension 0, may hold values from -12 to 12
- queries: bfloat16 [512, 1024], P(('groups', 'ref')), parts along dimension 0, may hold values from -48 to 48
- lengths: int32 [512], P(('groups', 'ref')), parts along dimension 0, may hold values from 512 to 1024, as said below
- groups: int32 [512], P(('groups', 'ref')), parts along dimension 0, may hold values from 0 to 127, as said below
Outputs:
- profile: float32 [512, 1024], P(('groups', 'ref')), parts along dimension 0
There are 2 independent parts, one for each index of `groups`. A program takes and returns all parts, laid end to end along the dimension named above; each array names one. Nothing has to cross between parts.
Inputs may be any that keep to these rules, and one draw needn't show every extreme that they name: `lengths`: multiples of 128. `groups`: region g holds reference blocks g * 1 to (g + 1) * 1 - 1; at most 4 queries name one region, and one region is named by exactly 4.
All inputs are finite; a program needn't handle non-finite values.
Results may differ from a plain program's by a relative error of at most 0.0003.
Values may be sent and summed in bfloat16 or wider, within the bound.
No kernel may reach another device: no remote copies, remote signals or barrier semaphores. Data moves between devices by JAX's collectives and lax.ppermute only.
A program may use at most 64 MiB of HBM per device.

v0:
```python
import jax
import jax.numpy as jnp
from jax import lax
from jax.sharding import PartitionSpec as P

M = 256
GDEV = 1
RMAX = 4


SPREAD_FLOOR = 0.25


def from_behind(block, axis, distance):
    devices = range(lax.axis_size(axis))
    route = [(i - distance, i) for i in devices if i - distance in devices]
    return lax.ppermute(block, axis, route)


def in_one_piece(arrays, axis, split_dim, concat_dim, along):
    columns = [a.reshape(*a.shape[:along], -1) for a in arrays]
    both = jnp.concatenate(columns, axis=along)
    result, at, outs = (
        lax.all_to_all(both, axis, split_axis=split_dim, concat_axis=concat_dim, tiled=True),
        0,
        [],
    )
    for a, column in zip(arrays, columns):
        section = result[..., at : at + column.shape[along]]
        outs.append(section.reshape(*section.shape[:along], *a.shape[along:]))
        at += column.shape[along]
    return tuple(outs)


def window_stats(series, count):
    total = series.shape[0]
    repeated = jnp.tile(series, (M + 1,))[: M * (total + 1)]
    windows = repeated.reshape(M, total + 1)[:, :count]
    values = windows.astype(jnp.float32)
    centre = jnp.mean(values, axis=0)
    spread = jnp.sqrt(jnp.mean((values - centre[None, :]) ** 2, axis=0) + SPREAD_FLOOR)
    return (windows, centre, spread)


def query_stats(series):
    return window_stats(jnp.concatenate([series, jnp.zeros((M,), jnp.bfloat16)]), series.shape[0])


def best_match(query_set, ref_set, usable):
    query_windows, query_centre, query_spread = query_set
    ref_windows, ref_centre, ref_spread = ref_set
    products = lax.dot_general(
        query_windows, ref_windows, (((0,), (0,)), ((), ())), preferred_element_type=jnp.float32
    )
    correlation = (products - M * query_centre[:, None] * ref_centre[None, :]) / (
        M * query_spread[:, None] * ref_spread[None, :]
    )
    correlation = jnp.where(usable[None, :], correlation, -2.0)
    return jnp.max(correlation, axis=1)


def body(long_series, queries, lengths, groups):
    members = lax.axis_size("ref")
    position = lax.axis_index("ref")
    per_device, series_len = queries.shape
    block_len = long_series.shape[0]
    overall = members * block_len
    leading = long_series[:M]
    trailing = from_behind(leading, "ref", -1)
    extended = jnp.concatenate([long_series, trailing])
    ref_set = window_stats(extended, block_len)
    usable = position * block_len + jnp.arange(block_len, dtype=jnp.int32) <= overall - M
    wanted = (jnp.arange(members, dtype=jnp.int32) // GDEV)[:, None] == groups[None, :]
    outgoing = jnp.where(wanted[:, :, None], queries[None, :, :], jnp.zeros((), jnp.bfloat16))
    arrived, slot_marks = in_one_piece((outgoing, wanted.astype(jnp.bfloat16)), "ref", 0, 0, 2)
    all_rows = arrived.reshape(members * per_device, series_len)
    live_slots = slot_marks.reshape(members * per_device) > 0.5
    slot_rank = jnp.cumsum(live_slots.astype(jnp.int32)) - 1
    chooser = jnp.logical_and(
        live_slots[None, :], slot_rank[None, :] == jnp.arange(RMAX, dtype=jnp.int32)[:, None]
    )
    compact = jnp.dot(
        chooser.astype(jnp.bfloat16), all_rows, preferred_element_type=jnp.float32
    ).astype(jnp.bfloat16)

    def match_row(series):
        return best_match(query_stats(series), ref_set, usable)

    found = lax.map(match_row, compact)
    spread_back = jnp.dot(
        chooser.astype(jnp.float32).T,
        found,
        precision=lax.Precision.HIGHEST,
        preferred_element_type=jnp.float32,
    )
    returned = lax.all_to_all(
        spread_back.reshape(members, per_device, series_len),
        "ref",
        split_axis=0,
        concat_axis=0,
        tiled=True,
    )
    best_values = jnp.max(jnp.where(wanted[:, :, None], returned, -2.0), axis=0)
    live_points = jnp.arange(series_len, dtype=jnp.int32)[None, :] <= lengths[:, None] - M
    return jnp.where(live_points, 2.0 * (1.0 - best_values), 0.0)


def solution(mesh):
    in_specs = (
        P(("groups", "ref")),
        P(("groups", "ref"), None),
        P(("groups", "ref")),
        P(("groups", "ref")),
    )
    out_specs = P(("groups", "ref"), None)
    return jax.shard_map(body, mesh=mesh, in_specs=in_specs, out_specs=out_specs, check_vma=False)
```

profile of v0, /device:TPU:513, one launch (start us, length us, event | category | flops | bytes accessed | tf_op | source)
XLA Modules:
  0.0 141.7 jit_solution(1548141993655549937)
XLA Ops:
  0.0 0.0 copy-start
  0.0 0.8 slice.38
  0.8 22.3 %collective-permute-start = (bf16[256]{0:T(256)(128)(2,1)S(1)}, bf16[256]{0:T(256)(128)(2,1)S(1)}, u32[]{:S(2)}, u32[]{:S(2)}) collective-permute-start(bf16[256]{0:T(256)(128)(2,1)S(1)} %slice.38), channel_id=1, source_target_pairs={{1,0},{2,1},{3,2},{4,3},{5,4},{6,5},{7,6},{8,7},{9,8},{10,9},{11,1... | collective-permute-start | bytes 1544 | tf_op jit(solution)/shard_map/ppermute | solution.py:17
  23.1 0.7 iota_compare_fusion
  23.8 0.8 compare_convert_fusion
  24.6 1.2 broadcast_select_fusion
  25.7 1.4 pad_maximum_fusion
  27.1 7.6 %all-to-all-start = ((bf16[128,2,1025]{2,1,0:T(2,128)(2,1)}), bf16[128,2,1025]{2,1,0:T(2,128)(2,1)S(1)}, u32[]{:S(2)}, u32[]{:S(2)}) async-start(bf16[128,2,1025]{2,1,0:T(2,128)(2,1)} %pad_maximum_fusion), calls=%async_computation | async-start | bytes 1179648 | tf_op jit(solution)/shard_map/all_to_all | solution.py:24
  34.8 0.0 collective-permute-done
  34.8 0.0 copy-done
  34.8 0.2 tile.24
  35.0 4.1 %tile.25 = bf16[1118464]{0:T(1024)(128)(2,1)} reshape(bf16[257,4352]{1,0:T(8,128)(2,1)S(1)} %tile.24) | data formatting | bytes 4473856 | tf_op jit(solution)/shard_map/tile | solution.py:37
  39.1 2.7 %slice.47 = bf16[1114368]{0:T(1024)(128)(2,1)} slice(bf16[1118464]{0:T(1024)(128)(2,1)} %tile.25), slice={[0:1114368]} | slice | bytes 4457472 | tf_op jit(solution)/shard_map/slice | solution.py:37
  41.8 5.4 %reshape.133 = bf16[256,4353]{1,0:T(8,128)(2,1)S(1)} reshape(bf16[1114368]{0:T(1024)(128)(2,1)} %slice.47) | data formatting | bytes 4457472 | tf_op jit(solution)/shard_map/reshape | solution.py:38
  47.1 1.6 %slice.48 = bf16[256,4096]{1,0:T(8,128)(2,1)} slice(bf16[256,4353]{1,0:T(8,128)(2,1)S(1)} %reshape.133), slice={[0:256], [0:4096]} | slice | bytes 4194304 | tf_op jit(solution)/shard_map/slice | solution.py:38
  48.7 0.3 convert_reduce_fusion.1
  49.1 0.6 fusion.6
  49.7 4.5 %all-to-all-done = bf16[128,2,1025]{2,1,0:T(2,128)(2,1)S(1)} async-done(((bf16[128,2,1025]{2,1,0:T(2,128)(2,1)}), bf16[128,2,1025]{2,1,0:T(2,128)(2,1)S(1)}, u32[]{:S(2)}, u32[]{:S(2)}) %all-to-all-start) | async-done | bytes 524832 | tf_op jit(solution)/shard_map/all_to_all | solution.py:24
  54.2 2.2 %fusion.7 = s32[128,2]{1,0:T(8,128)S(1)} fusion(bf16[128,2,1025]{2,1,0:T(2,128)(2,1)S(1)} %all-to-all-done), kind=kLoop, calls=%fused_computation.22 | loop fusion | flops 512 | bytes 1536 | tf_op jit(solution)/shard_map/convert_element_type | solution.py:78
  56.5 0.1 reshape.135
  56.6 0.3 reduce-window.9
  56.9 0.1 slice.35
  57.0 0.1 slice_reduce_fusion
  57.2 0.1 add_bitcast_fusion
  57.2 2.3 %compare_reduce_fusion = pred[128,2]{1,0:T(8,128)(4,1)S(1)} fusion(bf16[128,2,1025]{2,1,0:T(2,128)(2,1)S(1)} %all-to-all-done), kind=kLoop, calls=%fused_computation.21 | loop fusion | flops 256 | bytes 768 | tf_op jit(solution)/shard_map/gt | solution.py:77
  59.5 0.2 gt.17
  59.7 0.4 slice.46
  60.0 0.2 reshape.132
  60.2 0.2 convolution_convert_fusion
  60.4 37.3 %while.13 = (s32[]{:T(128)}, f32[4,1024]{1,0:T(4,128)S(1)}, bf16[4,1024]{1,0:T(4,128)(2,1)S(1)}, bf16[256,4096]{1,0:T(8,128)(2,1)}, f32[4096]{0:T(1024)S(1)}, /*...) while((s32[]{:T(128)}, f32[4,1024]{1,0:T(4,128)S(1)}, ...), condition=%wide.region_8.9_spmd.clone, body=%wide.region_4.8_spmd.clone.sunk | while | flops 2174231552 | bytes 8368755 | solution.py:89
  60.7 0.8 tile.31
  61.5 1.3 reshape.142
  62.7 0.1 convert_reduce_fusion.3
  62.9 0.2 fusion.24
  63.0 6.7 %select_reduce_fusion.3 = f32[1024]{0:T(1024)S(1)} fusion(bf16[256,4096]{1,0:T(8,128)(2,1)} %get-tuple-element.192, f32[4096]{0:T(1024)S(1)} %get-tuple-element.194, f32[1024]{0:T(1024)S(1)} %sqrt_multiply_fusion.2, f32[4096]{0:T(1024)S(1)} %get-tuple-element.193, f32[1024]{0:T(1024)S(1)} %convert_reduce_fusion.3, ...), kind=kOutput, calls=%fused_computation.1.clone.1 | convolution fusion | flops 2172648448 | bytes 2670592 | tf_op jit(solution)/shard_map/while/body/eval_jaxpr/dot_general | solution.py:52
  69.8 0.1 dynamic_update_slice.9
  70.0 0.8 tile.31
  70.8 1.3 reshape.142
  72.1 0.1 convert_reduce_fusion.3
  72.2 0.2 fusion.24
  72.3 6.7 %select_reduce_fusion.3 = f32[1024]{0:T(1024)S(1)} fusion(bf16[256,4096]{1,0:T(8,128)(2,1)} %get-tuple-element.192, f32[4096]{0:T(1024)S(1)} %get-tuple-element.194, f32[1024]{0:T(1024)S(1)} %sqrt_multiply_fusion.2, f32[4096]{0:T(1024)S(1)} %get-tuple-element.193, f32[1024]{0:T(1024)S(1)} %convert_reduce_fusion.3, ...), kind=kOutput, calls=%fused_computation.1.clone.1 | convolution fusion | flops 2172648448 | bytes 2670592 | tf_op jit(solution)/shard_map/while/body/eval_jaxpr/dot_general | solution.py:52
  79.1 0.1 dynamic_update_slice.9
  79.3 0.8 tile.31
  80.1 1.3 reshape.142
  81.3 0.1 convert_reduce_fusion.3
  81.5 0.2 fusion.24
  81.6 6.7 %select_reduce_fusion.3 = f32[1024]{0:T(1024)S(1)} fusion(bf16[256,4096]{1,0:T(8,128)(2,1)} %get-tuple-element.192, f32[4096]{0:T(1024)S(1)} %get-tuple-element.194, f32[1024]{0:T(1024)S(1)} %sqrt_multiply_fusion.2, f32[4096]{0:T(1024)S(1)} %get-tuple-element.193, f32[1024]{0:T(1024)S(1)} %convert_reduce_fusion.3, ...), kind=kOutput, calls=%fused_computation.1.clone.1 | convolution fusion | flops 2172648448 | bytes 2670592 | tf_op jit(solution)/shard_map/while/body/eval_jaxpr/dot_general | solution.py:52
  88.4 0.1 dynamic_update_slice.9
  88.6 0.8 tile.31
  89.4 1.3 reshape.142
  90.7 0.1 convert_reduce_fusion.3
  90.8 0.2 fusion.24
  91.0 6.7 %select_reduce_fusion.3 = f32[1024]{0:T(1024)S(1)} fusion(bf16[256,4096]{1,0:T(8,128)(2,1)} %get-tuple-element.192, f32[4096]{0:T(1024)S(1)} %get-tuple-element.194, f32[1024]{0:T(1024)S(1)} %sqrt_multiply_fusion.2, f32[4096]{0:T(1024)S(1)} %get-tuple-element.193, f32[1024]{0:T(1024)S(1)} %convert_reduce_fusion.3, ...), kind=kOutput, calls=%fused_computation.1.clone.1 | convolution fusion | flops 2172648448 | bytes 2670592 | tf_op jit(solution)/shard_map/while/body/eval_jaxpr/dot_general | solution.py:52
  97.7 0.1 dynamic_update_slice.9
  97.8 0.6 fusion.9
  98.4 0.0 copy-start.1
  98.4 1.6 %reshape.134 = f32[128,2,1024]{2,1,0:T(2,128)} reshape(f32[256,1024]{1,0:T(8,128)S(1)} %fusion.9) | data formatting | bytes 2097152 | tf_op jit(solution)/shard_map/reshape | solution.py:97
  100.0 10.8 %all-to-all-start.1 = ((f32[128,2,1024]{2,1,0:T(2,128)}), f32[128,2,1024]{2,1,0:T(2,128)S(1)}, u32[]{:S(2)}, u32[]{:S(2)}) async-start(f32[128,2,1024]{2,1,0:T(2,128)} %reshape.134), calls=%async_computation.1 | async-start | bytes 2097152 | tf_op jit(solution)/shard_map/all_to_all | solution.py:96
  110.9 0.0 copy-done.1
  110.9 29.6 %all-to-all-done.1 = f32[128,2,1024]{2,1,0:T(2,128)S(1)} async-done(((f32[128,2,1024]{2,1,0:T(2,128)}), f32[128,2,1024]{2,1,0:T(2,128)S(1)}, u32[]{:S(2)}, u32[]{:S(2)}) %all-to-all-start.1) | async-done | bytes 1048608 | tf_op jit(solution)/shard_map/all_to_all | solution.py:96
  140.5 0.5 select_reduce_fusion.1
  141.0 0.7 compare_select_fusion
  (34 shorter events, 0.7 us)
Async XLA Ops:
  0.0 34.8 %copy-start = (bf16[4096]{0:T(1024)(128)(2,1)S(1)}, bf16[4096]{0:T(1024)(128)(2,1)}, u32[]{:S(2)}) copy-start(bf16[4096]{0:T(1024)(128)(2,1)} %param.6) | copy-start | bytes 24580
  0.8 34.0 %collective-permute-start = (bf16[256]{0:T(256)(128)(2,1)S(1)}, bf16[256]{0:T(256)(128)(2,1)S(1)}, u32[]{:S(2)}, u32[]{:S(2)}) collective-permute-start(bf16[256]{0:T(256)(128)(2,1)S(1)} %slice.38), channel_id=1, source_target_pairs={{1,0},{2,1},{3,2},{4,3},{5,4},{6,5},{7,6},{8,7},{9,8},{10,9},{11,1... | collective-permute-start | bytes 1544 | tf_op jit(solution)/shard_map/ppermute | solution.py:17
  27.1 27.1 %all-to-all-start = ((bf16[128,2,1025]{2,1,0:T(2,128)(2,1)}), bf16[128,2,1025]{2,1,0:T(2,128)(2,1)S(1)}, u32[]{:S(2)}, u32[]{:S(2)}) async-start(bf16[128,2,1025]{2,1,0:T(2,128)(2,1)} %pad_maximum_fusion), calls=%async_computation | async-start | bytes 1179648 | tf_op jit(solution)/shard_map/all_to_all | solution.py:24
  98.4 12.5 %copy-start.1 = (s32[2]{0:T(128)S(1)}, s32[2]{0:T(128)}, u32[]{:S(2)}) copy-start(s32[2]{0:T(128)} %param.8) | copy-start | bytes 28
  100.0 40.5 %all-to-all-start.1 = ((f32[128,2,1024]{2,1,0:T(2,128)}), f32[128,2,1024]{2,1,0:T(2,128)S(1)}, u32[]{:S(2)}, u32[]{:S(2)}) async-start(f32[128,2,1024]{2,1,0:T(2,128)} %reshape.134), calls=%async_computation.1 | async-start | bytes 2097152 | tf_op jit(solution)/shard_map/all_to_all | solution.py:96
where the time goes:
time: 142 us
  starting transfers between devices  40.8 us (29%)
  waiting for transfers between devices  34.1 us (24%)
  matrix products  27.7 us (20%)
  local copies, waits for them, and re-layouts  26.3 us (19%)
  other arithmetic  12.2 us (9%)
    all_to_all x1, waiting for transfers between devices, body(): lax.all_to_all(spread_back.reshape(members, per_device, series_len), 'ref...  29.6 us
    dot_general x4, matrix products, best_match(): lax.dot_general(query_windows, ref_windows, (((0,), (0,)), ((), ())), pre...  26.8 us
    ppermute x1, starting transfers between devices, from_behind(): return lax.ppermute(block, axis, route)  22.3 us
    all_to_all x1, starting transfers between devices, body(): lax.all_to_all(spread_back.reshape(members, per_device, series_len), 'ref...  10.8 us
    reshape x5, local copies, waits for them, and re-layouts, window_stats(): windows = repeated.reshape(M, total + 1)[:, :count]  10.4 us
    all_to_all x1, starting transfers between devices, in_one_piece(): lax.all_to_all(both, axis, split_axis=split_dim, concat_axis=concat_dim,...  7.64 us
    another operation x10, local copies, waits for them, and re-layouts, window_stats(): repeated = jnp.tile(series, (M + 1,))[:M * (total + 1)]  7.49 us
    all_to_all x1, waiting for transfers between devices, in_one_piece(): lax.all_to_all(both, axis, split_axis=split_dim, concat_axis=concat_dim,...  4.54 us
  transfers between devices with their start and end apart: 3, of which 2 were waited for; matrix products, arithmetic and copies ran while one was open for 13% of the time, Pallas kernels for 0%

commit v1 on v0

v1 whole, which is shorter than its diff:
```python
import functools
import math

import jax
import jax.numpy as jnp
from jax import lax
from jax.experimental import pallas as pl
from jax.experimental.pallas import tpu as pltpu
from jax.sharding import Mesh
from jax.sharding import PartitionSpec as P


M = 256
LANES = 128
SPREAD_FLOOR = 0.25
CORES = 2
NEVER = -3.0e38


def lane_iota(rows):
    return lax.broadcasted_iota(jnp.int32, (rows, LANES), 1)


def ahead(x, n, width):
    rows = x.shape[0]
    below = pltpu.roll(x, rows - 1, axis=0)
    if n == width:
        return below
    lane = lane_iota(rows)
    return jnp.where(lane < width - n, pltpu.roll(x, width - n, axis=1), pltpu.roll(below, width - n, axis=1))


def window_stats(x):
    total = x
    squares = jnp.zeros_like(x)
    n = 1
    while n < M:
        other = ahead(total, n, LANES)
        apart = total - other
        squares = squares + apart * apart * (0.5 / n)
        if n > 1:
            squares = squares + ahead(merged, n, LANES)
        merged = squares
        total = total + other
        n *= 2
    centre = total * (1.0 / M)
    spread = jnp.sqrt(squares * (1.0 / M) + SPREAD_FLOOR)
    return centre, spread


def hankel_rows(rows_of, blocks, put):
    sub = lax.broadcasted_iota(jnp.int32, (8, LANES), 0)
    lane = lane_iota(8)

    def rolled(b):
        base = jnp.broadcast_to(rows_of(b), (8, LANES))
        for bit in (1, 2, 4):
            base = jnp.where((sub & bit) != 0, pltpu.roll(base, LANES - bit, axis=1), base)
        return [base] + [pltpu.roll(base, LANES - 8 * t, axis=1) for t in range(1, LANES // 8)]

    own = rolled(0)
    for b in range(blocks):
        after = rolled(b + 1)
        pieces = [
            jnp.where(lane + sub < LANES - 8 * t, own[t], after[t]) for t in range(LANES // 8)
        ]
        put(b, jnp.concatenate(pieces, axis=0).astype(jnp.bfloat16))
        own = after


def prepare_queries(queries_ref, windows_ref, centre_ref, scale_ref):
    count, length = queries_ref.shape
    rows = length // LANES
    zero = jnp.zeros((1, LANES), jnp.float32)
    for s in range(count):
        parts = [
            queries_ref[s : s + 1, LANES * b : LANES * (b + 1)].astype(jnp.float32)
            for b in range(rows)
        ]

        def put(b, tile, s=s):
            windows_ref[s, LANES * b : LANES * (b + 1), :] = tile

        hankel_rows(lambda b: parts[b] if b < rows else zero, rows + 1, put)
        series = jnp.concatenate(parts + [zero] * 8, axis=0)
        centre, spread = window_stats(series)
        scale_ref[s] = 1.0 / (M * spread[:rows])
        for b in range(rows):
            wide = jnp.broadcast_to(centre[b : b + 1], (LANES, LANES))
            centre_ref[s, LANES * b : LANES * (b + 1), :] = wide.T


def answer(position_ref, *refs):
    *requests, blocks_ref, replies_ref = refs
    held, rows, _ = blocks_ref.shape
    peers, slots = len(requests), requests[0].shape[0]
    for distance, request in enumerate(requests):
        p = lax.rem(position_ref[0] + peers - distance, peers)
        for s in range(slots):
            want = lax.rem(request[s], held)
            follow = jnp.minimum(want + 1, held - 1)
            replies_ref[p, rows * s : rows * (s + 1), :] = blocks_ref[want]
            replies_ref[p, rows * slots + 8 * s : rows * slots + 8 * (s + 1), :] = blocks_ref[follow, 0:8, :]
        replies_ref[p, rows * slots + 8 * slots : rows * slots + 8 * slots + 8, :] = blocks_ref[0, 0:8, :]


def join(held, overall, groups_ref, lengths_ref, replies_ref, windows_ref, centre_ref, scale_ref, out_ref, ref_windows, weights, running):
    peers = replies_ref.shape[0]
    slots = groups_ref.shape[0]
    rows = (replies_ref.shape[1] - 8 * slots - 8) // slots
    block_len = rows * LANES
    query_len = centre_ref.shape[1]
    chunk = min(256, query_len)
    for s in range(slots):
        region = groups_ref[s]
        column = region // held
        place = lax.rem(region, held)
        block = replies_ref[column, rows * s : rows * (s + 1), :].astype(jnp.float32)
        inside = replies_ref[column, rows * slots + 8 * s : rows * slots + 8 * (s + 1), :]
        beyond = replies_ref[lax.rem(column + 1, peers), rows * slots + 8 * slots : rows * slots + 8 * slots + 8, :]
        halo = jnp.where(place == held - 1, beyond.astype(jnp.float32), inside.astype(jnp.float32))
        series = jnp.concatenate([block, halo], axis=0)

        def put(b, tile):
            ref_windows[LANES * b : LANES * (b + 1), :] = tile

        hankel_rows(lambda b: series[b : b + 1], rows + 1, put)
        centre, spread = window_stats(series)
        inverse = 1.0 / spread[:rows]
        weights[0, :, :] = inverse
        weights[1, :, :] = (M * centre[:rows]) * inverse
        start = region * block_len + lax.broadcasted_iota(jnp.int32, (rows, LANES), 0) * LANES + lane_iota(rows)
        weights[2, :, :] = jnp.where(start <= overall - M, 0.0, NEVER)
        running[...] = jnp.full(running.shape, NEVER, jnp.float32)

        def step(t, carry):
            j = pl.multiple_of(t * M, M)
            tile = jnp.concatenate([ref_windows[pl.ds(j, M), :], ref_windows[pl.ds(j + LANES, M), :]], axis=1)
            left = [jnp.broadcast_to(weights[k, pl.ds(2 * t, 1), :], (8, LANES)) for k in range(3)]
            right = [jnp.broadcast_to(weights[k, pl.ds(2 * t + 1, 1), :], (8, LANES)) for k in range(3)]
            for i in range(0, query_len, chunk):
                lhs = jnp.concatenate([windows_ref[s, i : i + chunk, :], windows_ref[s, i + LANES : i + LANES + chunk, :]], axis=1)
                products = jnp.dot(lhs, tile, preferred_element_type=jnp.float32)
                for r in range(0, chunk, 8):
                    mean = centre_ref[s, i + r : i + r + 8, :]
                    one = products[r : r + 8, :LANES] * left[0] - mean * left[1] + left[2]
                    two = products[r : r + 8, LANES:] * right[0] - mean * right[1] + right[2]
                    running[i + r : i + r + 8, :] = jnp.maximum(running[i + r : i + r + 8, :], jnp.maximum(one, two))
            return carry

        lax.fori_loop(0, block_len // M, step, 0)
        for b in range(query_len // LANES):
            best = jnp.max(running[LANES * b : LANES * (b + 1), :].T, axis=0, keepdims=True)
            best = best * scale_ref[s, b : b + 1, :]
            place_of = LANES * b + lane_iota(1)
            out_ref[s : s + 1, LANES * b : LANES * (b + 1)] = jnp.where(
                place_of <= lengths_ref[s] - M, 2.0 * (1.0 - best), 0.0
            )


VMEM = pl.BlockSpec(memory_space=pltpu.VMEM)
SMEM = pl.BlockSpec(memory_space=pltpu.SMEM)


def call(kernel, out_shape, in_specs, scratch=(), limit=8 << 20):
    many = isinstance(out_shape, tuple)
    return pl.pallas_call(
        kernel,
        out_shape=out_shape,
        in_specs=in_specs,
        out_specs=(VMEM,) * len(out_shape) if many else VMEM,
        scratch_shapes=scratch,
        compiler_params=pltpu.CompilerParams(vmem_limit_bytes=limit),
    )


def body(long_series, queries, lengths, groups):
    slots, query_len = queries.shape
    rows = long_series.shape[0] // LANES
    across, along = lax.axis_size("x"), lax.axis_size("y") * CORES
    overall = across * along * long_series.shape[0]
    asked = [groups] + [
        lax.ppermute(groups, "x", [(i, (i + d) % across) for i in range(across)]) for d in range(1, across)
    ]
    block = long_series.reshape(rows, LANES)
    gathered = lax.all_to_all(
        jnp.broadcast_to(block, (along, rows, LANES)), ("y", "core"), 0, 0, tiled=True
    )
    windows, centre, scale = call(
        prepare_queries,
        (
            jax.ShapeDtypeStruct((slots, query_len + LANES, LANES), jnp.bfloat16),
            jax.ShapeDtypeStruct((slots, query_len, LANES), jnp.float32),
            jax.ShapeDtypeStruct((slots, query_len // LANES, LANES), jnp.float32),
        ),
        [VMEM],
    )(queries)
    replies = call(
        answer,
        jax.ShapeDtypeStruct((across, rows * slots + 8 * slots + 8, LANES), jnp.bfloat16),
        [SMEM] * (1 + across) + [VMEM],
    )(lax.axis_index("x").reshape(1), *asked, gathered)
    received = lax.all_to_all(replies, "x", 0, 0, tiled=True)
    return call(
        functools.partial(join, along, overall),
        jax.ShapeDtypeStruct((slots, query_len), jnp.float32),
        [SMEM, SMEM, VMEM, VMEM, VMEM, VMEM],
        [
            pltpu.VMEM(((rows + 1) * LANES, LANES), jnp.bfloat16),
            pltpu.VMEM((3, rows, LANES), jnp.float32),
            pltpu.VMEM((query_len, LANES), jnp.float32),
        ],
    )(groups, lengths, received, windows, centre, scale)


def solution(mesh):
    outer, members = mesh.devices.shape
    side = math.isqrt(members // CORES)
    plane = Mesh(
        mesh.devices.reshape(outer, members // CORES // side, side, CORES), ("groups", "x", "y", "core")
    )
    every = ("groups", "x", "y", "core")
    return jax.shard_map(
        body,
        mesh=plane,
        in_specs=(P(every), P(every, None), P(every), P(every)),
        out_specs=P(every, None),
        check_vma=False,
    )
```

time: 142 us -> 73.8 us (0.52)
  the two profiles are of different devices: /device:TPU:513 before, /device:TPU:514 now
where the time goes in v1:
time: 73.8 us; the launch traced here: 73.4 us
  starting transfers between devices  40.2 us (54%)
  Pallas kernels  20.6 us (28%)
  waiting for transfers between devices  10.6 us (14%)
  local copies, waits for them, and re-layouts  2.03 us (3%)
    ppermute x7, starting transfers between devices, body(): lax.ppermute(groups, 'x', [(i, (i + d) % across) for i in range(across)])  19.4 us
    pallas_call x1, Pallas kernels, body(): call(functools.partial(join, along, overall), jax.ShapeDtypeStruct((slots...  18.1 us
    all_to_all x1, starting transfers between devices, body(): lax.all_to_all(jnp.broadcast_to(block, (along, rows, LANES)), ('y', 'core...  13.6 us
    all_to_all x1, starting transfers between devices, body(): received = lax.all_to_all(replies, 'x', 0, 0, tiled=True)  7.15 us
    all_to_all x1, waiting for transfers between devices, body(): received = lax.all_to_all(replies, 'x', 0, 0, tiled=True)  6.95 us
    ppermute x7, waiting for transfers between devices, body(): lax.ppermute(groups, 'x', [(i, (i + d) % across) for i in range(across)])  3.65 us
  transfers between devices with their start and end apart: 9, of which 3 were waited for; matrix products, arithmetic and copies ran while one was open for 0% of the time, Pallas kernels for 2%

profile of v1, /device:TPU:514, one launch (start us, length us, event | category | flops | bytes accessed | tf_op | source)
XLA Modules:
  0.0 73.4 jit_solution(14310951602293258347)
XLA Ops:
  0.0 1.4 %broadcast_in_dim.3 = bf16[16,32,128]{2,1,0:T(8,128)(2,1)} broadcast(bf16[32,128]{1,0:T(8,128)(2,1)} %bitcast.2), dimensions={1,2} | broadcast | bytes 139264 | tf_op jit(solution)/shard_map/broadcast_in_dim | solution.py:187
  1.4 0.0 copy-start.1
  1.4 13.6 %all-to-all-start = ((bf16[16,32,128]{2,1,0:T(8,128)(2,1)}), bf16[16,32,128]{2,1,0:T(8,128)(2,1)S(1)}, u32[]{:S(2)}, u32[]{:S(2)}) async-start(bf16[16,32,128]{2,1,0:T(8,128)(2,1)} %broadcast_in_dim.3), calls=%async_computation | async-start | bytes 262144 | tf_op jit(solution)/shard_map/all_to_all | solution.py:186
  15.0 0.0 copy-done.1
  15.0 10.0 %collective-permute-start.6 = (s32[2]{0:T(128)S(1)}, s32[2]{0:T(128)S(1)}, u32[]{:S(2)}, u32[]{:S(2)}) collective-permute-start(s32[2]{0:T(128)S(1)} %copy-done.1), channel_id=1, source_target_pairs={{0,112},{16,0},{32,16},{48,32},{64,48},{80,64},{96,80},{112,96},{1... | collective-permute-start | bytes 32 | tf_op jit(solution)/shard_map/ppermute | solution.py:183
  25.0 0.0 collective-permute-start.5
  25.0 0.0 collective-permute-start.4
  25.0 6.1 %collective-permute-start.3 = (s32[2]{0:T(128)S(1)}, s32[2]{0:T(128)S(1)}, u32[]{:S(2)}, u32[]{:S(2)}) collective-permute-start(s32[2]{0:T(128)S(1)} %copy-done.1), channel_id=1, source_target_pairs={{0,64},{16,80},{32,96},{48,112},{64,0},{80,16},{96,32},{112,48},{1... | collective-permute-start | bytes 32 | tf_op jit(solution)/shard_map/ppermute | solution.py:183
  31.0 0.0 collective-permute-start.2
  31.0 0.0 collective-permute-done.6.refs_7_
  31.0 1.9 %collective-permute-start.1 = (s32[2]{0:T(128)S(1)}, s32[2]{0:T(128)S(1)}, u32[]{:S(2)}, u32[]{:S(2)}) collective-permute-start(s32[2]{0:T(128)S(1)} %copy-done.1), channel_id=1, source_target_pairs={{0,32},{16,48},{32,64},{48,80},{64,96},{80,112},{96,0},{112,16},{1... | collective-permute-start | bytes 32 | tf_op jit(solution)/shard_map/ppermute | solution.py:183
  32.9 0.0 collective-permute-done.5.refs_6_
  32.9 1.5 %collective-permute-start = (s32[2]{0:T(128)S(1)}, s32[2]{0:T(128)S(1)}, u32[]{:S(2)}, u32[]{:S(2)}) collective-permute-start(s32[2]{0:T(128)S(1)} %copy-done.1), channel_id=1, source_target_pairs={{0,16},{16,32},{32,48},{48,64},{64,80},{80,96},{96,112},{112,0},{1... | collective-permute-start | bytes 32 | tf_op jit(solution)/shard_map/ppermute | solution.py:183
  34.4 0.0 collective-permute-done.4.refs_5_
  34.4 0.0 collective-permute-done.3.refs_4_
  34.4 3.2 %collective-permute-done.2.refs_3_ = s32[2]{0:T(128)S(1)} collective-permute-done((s32[2]{0:T(128)S(1)}, s32[2]{0:T(128)S(1)}, u32[]{:S(2)}, u32[]{:S(2)}) %collective-permute-start.2) | collective-permute-done | bytes 40 | tf_op jit(solution)/shard_map/ppermute | solution.py:183
  37.6 0.4 collective-permute-done.1.refs_2_
  38.0 0.0 collective-permute-done.refs_1_
  38.1 0.0 all-to-all-done.refs_8_
  38.1 1.3 %shard_map.46 = bf16[8,88,128]{2,1,0:T(8,128)(2,1)} custom-call(s32[1]{0:T(128)} %bitcast.position_ref, s32[2]{0:T(128)S(1)} %copy-done.1, s32[2]{0:T(128)S(1)} %collective-permute-done.refs_1_, s32[2]{0:T(128)S(1)} %collective-permute-done.1.refs_2_, s32[2]{0:T(128)S(1)} %collective-permute-done.2.refs_3_, s32[2]{0:T(128)S(1)} %collective-permute-done.3.refs_4_, ...), custom_call_target="tpu_custom_call" | custom-call | tf_op jit(solution)/shard_map/pallas_call | solution.py:198
  39.4 0.0 copy-start
  39.4 7.2 %all-to-all-start.1 = ((bf16[8,88,128]{2,1,0:T(8,128)(2,1)}), bf16[8,88,128]{2,1,0:T(8,128)(2,1)S(1)}, u32[]{:S(2)}, u32[]{:S(2)}) async-start(bf16[8,88,128]{2,1,0:T(8,128)(2,1)} %shard_map.46), calls=%async_computation.1 | async-start | bytes 360448 | tf_op jit(solution)/shard_map/all_to_all | solution.py:203
  46.6 0.0 copy-done
  46.6 1.1 %shard_map.47 = (bf16[2,1152,128]{2,1,0:T(8,128)(2,1)S(1)}, f32[2,1024,128]{2,1,0:T(8,128)S(1)}, f32[2,8,128]{2,1,0:T(8,128)S(1)}) custom-call(bf16[2,1024]{1,0:T(2,128)(2,1)S(1)} %copy-done), custom_call_target="tpu_custom_call" | custom-call | tf_op jit(solution)/shard_map/pallas_call | solution.py:189
  47.7 6.9 %all-to-all-done.1.replies_ref = bf16[8,88,128]{2,1,0:T(8,128)(2,1)S(1)} async-done(((bf16[8,88,128]{2,1,0:T(8,128)(2,1)}), bf16[8,88,128]{2,1,0:T(8,128)(2,1)S(1)}, u32[]{:S(2)}, u32[]{:S(2)}) %all-to-all-start.1) | async-done | bytes 180256 | tf_op jit(solution)/shard_map/all_to_all | solution.py:203
  54.6 0.0 copy-start.2
  54.6 0.7 copy-done.2
  55.3 18.1 %shard_map.48 = f32[2,1024]{1,0:T(2,128)} custom-call(s32[2]{0:T(128)S(1)} %copy-done.1, s32[2]{0:T(128)S(1)} %copy-done.2, bf16[8,88,128]{2,1,0:T(8,128)(2,1)S(1)} %all-to-all-done.1.replies_ref, bf16[2,1152,128]{2,1,0:T(8,128)(2,1)S(1)} %get-tuple-element.8.windows_ref, f32[2,1024,128]{2,1,0:T(8,128)S(1)} %get-tuple-element.9.centre_ref, ...), custom_call_target="tpu_custom_call" | custom-call | tf_op jit(solution)/shard_map/pallas_call | solution.py:204
Async XLA Ops:
  1.4 13.6 %copy-start.1 = (s32[2]{0:T(128)S(1)}, s32[2]{0:T(128)}, u32[]{:S(2)}) copy-start(s32[2]{0:T(128)} %groups_ref.1) | copy-start | bytes 28
  1.4 36.7 %all-to-all-start = ((bf16[16,32,128]{2,1,0:T(8,128)(2,1)}), bf16[16,32,128]{2,1,0:T(8,128)(2,1)S(1)}, u32[]{:S(2)}, u32[]{:S(2)}) async-start(bf16[16,32,128]{2,1,0:T(8,128)(2,1)} %broadcast_in_dim.3), calls=%async_computation | async-start | bytes 262144 | tf_op jit(solution)/shard_map/all_to_all | solution.py:186
  15.0 16.1 %collective-permute-start.6 = (s32[2]{0:T(128)S(1)}, s32[2]{0:T(128)S(1)}, u32[]{:S(2)}, u32[]{:S(2)}) collective-permute-start(s32[2]{0:T(128)S(1)} %copy-done.1), channel_id=1, source_target_pairs={{0,112},{16,0},{32,16},{48,32},{64,48},{80,64},{96,80},{112,96},{1... | collective-permute-start | bytes 32 | tf_op jit(solution)/shard_map/ppermute | solution.py:183
  25.0 8.0 %collective-permute-start.5 = (s32[2]{0:T(128)S(1)}, s32[2]{0:T(128)S(1)}, u32[]{:S(2)}, u32[]{:S(2)}) collective-permute-start(s32[2]{0:T(128)S(1)} %copy-done.1), channel_id=1, source_target_pairs={{0,96},{16,112},{32,0},{48,16},{64,32},{80,48},{96,64},{112,80},{1... | collective-permute-start | bytes 32 | tf_op jit(solution)/shard_map/ppermute | solution.py:183
  25.0 9.4 %collective-permute-start.4 = (s32[2]{0:T(128)S(1)}, s32[2]{0:T(128)S(1)}, u32[]{:S(2)}, u32[]{:S(2)}) collective-permute-start(s32[2]{0:T(128)S(1)} %copy-done.1), channel_id=1, source_target_pairs={{0,80},{16,96},{32,112},{48,0},{64,16},{80,32},{96,48},{112,64},{1... | collective-permute-start | bytes 32 | tf_op jit(solution)/shard_map/ppermute | solution.py:183
  25.0 9.4 %collective-permute-start.3 = (s32[2]{0:T(128)S(1)}, s32[2]{0:T(128)S(1)}, u32[]{:S(2)}, u32[]{:S(2)}) collective-permute-start(s32[2]{0:T(128)S(1)} %copy-done.1), channel_id=1, source_target_pairs={{0,64},{16,80},{32,96},{48,112},{64,0},{80,16},{96,32},{112,48},{1... | collective-permute-start | bytes 32 | tf_op jit(solution)/shard_map/ppermute | solution.py:183
  31.0 6.6 %collective-permute-start.2 = (s32[2]{0:T(128)S(1)}, s32[2]{0:T(128)S(1)}, u32[]{:S(2)}, u32[]{:S(2)}) collective-permute-start(s32[2]{0:T(128)S(1)} %copy-done.1), channel_id=1, source_target_pairs={{0,48},{16,64},{32,80},{48,96},{64,112},{80,0},{96,16},{112,32},{1... | collective-permute-start | bytes 32 | tf_op jit(solution)/shard_map/ppermute | solution.py:183
  31.0 7.0 %collective-permute-start.1 = (s32[2]{0:T(128)S(1)}, s32[2]{0:T(128)S(1)}, u32[]{:S(2)}, u32[]{:S(2)}) collective-permute-start(s32[2]{0:T(128)S(1)} %copy-done.1), channel_id=1, source_target_pairs={{0,32},{16,48},{32,64},{48,80},{64,96},{80,112},{96,0},{112,16},{1... | collective-permute-start | bytes 32 | tf_op jit(solution)/shard_map/ppermute | solution.py:183
  32.9 5.1 %collective-permute-start = (s32[2]{0:T(128)S(1)}, s32[2]{0:T(128)S(1)}, u32[]{:S(2)}, u32[]{:S(2)}) collective-permute-start(s32[2]{0:T(128)S(1)} %copy-done.1), channel_id=1, source_target_pairs={{0,16},{16,32},{32,48},{48,64},{64,80},{80,96},{96,112},{112,0},{1... | collective-permute-start | bytes 32 | tf_op jit(solution)/shard_map/ppermute | solution.py:183
  39.4 7.2 %copy-start = (bf16[2,1024]{1,0:T(2,128)(2,1)S(1)}, bf16[2,1024]{1,0:T(2,128)(2,1)}, u32[]{:S(2)}) copy-start(bf16[2,1024]{1,0:T(2,128)(2,1)} %queries_ref.1) | copy-start | bytes 12292
  39.4 15.2 %all-to-all-start.1 = ((bf16[8,88,128]{2,1,0:T(8,128)(2,1)}), bf16[8,88,128]{2,1,0:T(8,128)(2,1)S(1)}, u32[]{:S(2)}, u32[]{:S(2)}) async-start(bf16[8,88,128]{2,1,0:T(8,128)(2,1)} %shard_map.46), calls=%async_computation.1 | async-start | bytes 360448 | tf_op jit(solution)/shard_map/all_to_all | solution.py:203
  54.6 0.7 copy-start.2

commit v2 on v1

v2 whole, which is shorter than its diff:
```python
import functools

import jax
import jax.numpy as jnp
from jax import lax
from jax.experimental import pallas as pl
from jax.experimental.pallas import tpu as pltpu
from jax.sharding import Mesh
from jax.sharding import PartitionSpec as P


M = 256
LANES = 128
SPREAD_FLOOR = 0.25
CORES = 2
NEVER = -3.0e38
PIECE = 64
LAG = 8


def lane_iota(rows):
    return lax.broadcasted_iota(jnp.int32, (rows, LANES), 1)


def ahead(x, n, width):
    rows = x.shape[0]
    below = pltpu.roll(x, rows - 1, axis=0)
    if n == width:
        return below
    lane = lane_iota(rows)
    return jnp.where(lane < width - n, pltpu.roll(x, width - n, axis=1), pltpu.roll(below, width - n, axis=1))


def window_stats(x):
    total = x
    squares = jnp.zeros_like(x)
    n = 1
    while n < M:
        other = ahead(total, n, LANES)
        apart = total - other
        squares = squares + apart * apart * (0.5 / n)
        if n > 1:
            squares = squares + ahead(merged, n, LANES)
        merged = squares
        total = total + other
        n *= 2
    centre = total * (1.0 / M)
    spread = jnp.sqrt(squares * (1.0 / M) + SPREAD_FLOOR)
    return centre, spread


class Hankel:
    def __init__(self, rows_of):
        self.rows_of = rows_of
        self.sub = lax.broadcasted_iota(jnp.int32, (8, LANES), 0)
        self.lane = lane_iota(8)
        self.kept = {}

    def rolled(self, b):
        if b not in self.kept:
            base = jnp.broadcast_to(self.rows_of(b), (8, LANES))
            for bit in (1, 2, 4):
                base = jnp.where((self.sub & bit) != 0, pltpu.roll(base, LANES - bit, axis=1), base)
            self.kept[b] = [base] + [pltpu.roll(base, LANES - 8 * t, axis=1) for t in range(1, LANES // 8)]
        return self.kept[b]

    def tile(self, b):
        own, after = self.rolled(b), self.rolled(b + 1)
        pieces = [
            jnp.where(self.lane + self.sub < LANES - 8 * t, own[t], after[t]) for t in range(LANES // 8)
        ]
        return jnp.concatenate(pieces, axis=0).astype(jnp.bfloat16)


def prepare_queries(queries_ref, windows_ref, centre_ref, scale_ref):
    count, length = queries_ref.shape
    rows = length // LANES
    zero = jnp.zeros((1, LANES), jnp.float32)
    for s in range(count):
        parts = [
            queries_ref[s : s + 1, LANES * b : LANES * (b + 1)].astype(jnp.float32)
            for b in range(rows)
        ]
        padded = parts + [zero] * 2
        hankel = Hankel(lambda b: padded[b])
        for b in range(rows + 1):
            windows_ref[s, LANES * b : LANES * (b + 1), :] = hankel.tile(b)
        series = jnp.concatenate(parts + [zero] * 8, axis=0)
        centre, spread = window_stats(series)
        scale_ref[s] = 1.0 / (M * spread[:rows])
        for b in range(rows):
            wide = jnp.broadcast_to(centre[b : b + 1], (LANES, LANES))
            centre_ref[s, LANES * b : LANES * (b + 1), :] = wide.T


def pick(theirs_ref, gathered_ref, out_ref):
    held, rows, _ = gathered_ref.shape
    slots = theirs_ref.shape[0]
    for s in range(slots):
        want = theirs_ref[s]
        out_ref[rows * s : rows * (s + 1), :] = gathered_ref[want // CORES]
        follow = jnp.minimum((want + 1) // CORES, held - 1)
        out_ref[rows * slots + 8 * s : rows * slots + 8 * (s + 1), :] = gathered_ref[follow, 0:8, :]


def join(overall, core_ref, groups_ref, lengths_ref, gathered_ref, passed_ref, windows_ref, centre_ref, scale_ref, out_ref, ref_windows, weights, running, series):
    held, rows, _ = gathered_ref.shape
    slots = groups_ref.shape[0]
    block_len = rows * LANES
    query_len = centre_ref.shape[1]
    parts = []
    for s in range(slots):
        region = groups_ref[s]
        follow = jnp.minimum((region + 1) // CORES, held - 1)
        block = jnp.where(
            lax.rem(region, CORES) == core_ref[0],
            gathered_ref[region // CORES].astype(jnp.float32),
            passed_ref[rows * s : rows * (s + 1), :].astype(jnp.float32),
        )
        halo = jnp.where(
            lax.rem(region + 1, CORES) == core_ref[0],
            gathered_ref[follow, 0:8, :].astype(jnp.float32),
            passed_ref[rows * slots + 8 * s : rows * slots + 8 * (s + 1), :].astype(jnp.float32),
        )
        parts.append(jnp.concatenate([block, halo], axis=0))
        series[s] = parts[s]
    centre, spread = window_stats(jnp.concatenate(parts, axis=0))
    inverse = 1.0 / spread
    factor = [inverse, (M * centre) * inverse]
    for s in range(slots):
        start = groups_ref[s] * block_len + LANES * lax.broadcasted_iota(jnp.int32, (rows + 8, LANES), 0) + lane_iota(rows + 8)
        for w in range(2):
            own = factor[w][(rows + 8) * s : (rows + 8) * (s + 1)]
            same = own[rows - M // LANES : rows - M // LANES + 1, 0:1]
            weights[w, (rows + 8) * s : (rows + 8) * (s + 1), :] = jnp.where(start <= overall - M, own, same)

    trips = block_len // (2 * M)
    pieces = query_len // PIECE
    tail = block_len - M

    def compute(*accs):
        def push(u):
            s, t = u // trips, u % trips
            for q in range(2):
                tile = []
                for h in range(2):
                    j = 2 * M * t + M * q + LANES * h
                    if q:
                        j = jnp.where(t == trips - 1, block_len + LANES + M * h, j)
                    tile.append(ref_windows[s, pl.ds(pl.multiple_of(j, LANES), M), :])
                pltpu.matmul_push_rhs(jnp.concatenate(tile, axis=1), staging_register=0, mxu_index=q)

        def factors(u):
            top = (rows + 8) * (u // trips) + 4 * (u % trips)
            return [
                [jnp.broadcast_to(weights[w, pl.ds(top + k, 1), :], (8, LANES)) for k in range(4)] for w in range(2)
            ]

        def drain(u, n, scale, shift):
            s = u // trips
            both = [pltpu.matmul_pop(accs[2 * n + q]) for q in range(2)]
            for r in range(0, PIECE, 8):
                at = PIECE * n + r
                mean = centre_ref[s, at : at + 8, :]
                found = [
                    both[k // 2][r : r + 8, LANES * (k % 2) : LANES * (k % 2 + 1)] * scale[k] - mean * shift[k]
                    for k in range(4)
                ]
                best = jnp.maximum(jnp.maximum(found[0], found[1]), jnp.maximum(found[2], found[3]))
                running[s, at : at + 8, :] = jnp.maximum(running[s, at : at + 8, :], best)

        def trip(u, first, last):
            s = u // trips
            before = None if first else factors(u - 1)
            now = factors(u)
            for n in range(pieces):
                i = PIECE * n
                lhs = jnp.concatenate(
                    [windows_ref[s, i : i + PIECE, :], windows_ref[s, i + LANES : i + LANES + PIECE, :]], axis=1
                )
                if n >= LAG:
                    drain(u, n - LAG, *now)
                elif not first:
                    drain(u - 1, pieces + n - LAG, *before)
                for q in range(2):
                    pltpu.matmul_acc_lhs(accs[2 * n + q], lhs, load_staged_rhs=0 if n == 0 else None)
                if n == 0 and not last:
                    push(u + 1)
            if last:
                for n in range(pieces - LAG, pieces):
                    drain(u, n, *now)

        for acc in accs:
            pltpu.matmul_pop(acc)
        push(0)
        trip(0, True, False)

        def middle(u, carry):
            trip(u, False, False)
            return carry

        lax.fori_loop(1, slots * trips - 1, middle, 0)
        trip(slots * trips - 1, False, True)

    running[...] = jnp.full(running.shape, NEVER, jnp.float32)
    for s in range(slots):
        hankel = Hankel(lambda b: series[s, b : b + 1, :])
        for b in range(rows + 1):
            tile = hankel.tile(b)
            ref_windows[s, LANES * b : LANES * (b + 1), :] = tile
            for h in range(4):
                if LANES * (b - h + h // 2) == tail:
                    at = block_len + LANES * (h + 1)
                    ref_windows[s, at : at + LANES, :] = tile
    for s in range(slots):

        @pl.when(groups_ref[s] * block_len + tail + LANES > overall - M)
        def _(s=s):
            for h in range(4):
                row = series[s, tail // LANES + h % 2 : tail // LANES + h % 2 + 1, :]
                same = jnp.broadcast_to(row, (LANES, LANES)).T.astype(jnp.bfloat16)
                at = block_len + LANES * (h + 1)
                ref_windows[s, at : at + LANES, :] = same

    pl.run_scoped(
        compute,
        *[pltpu.ACC(n % 2)((PIECE, 2 * LANES), jnp.float32) for n in range(2 * pieces)],
    )
    for s in range(slots):
        for b in range(query_len // LANES):
            best = jnp.max(running[s, LANES * b : LANES * (b + 1), :].T, axis=0, keepdims=True)
            best = best * scale_ref[s, b : b + 1, :]
            place_of = LANES * b + lane_iota(1)
            out_ref[s : s + 1, LANES * b : LANES * (b + 1)] = jnp.where(
                place_of <= lengths_ref[s] - M, 2.0 * (1.0 - best), 0.0
            )


VMEM = pl.BlockSpec(memory_space=pltpu.VMEM)
SMEM = pl.BlockSpec(memory_space=pltpu.SMEM)


def call(kernel, out_shape, in_specs, scratch=(), limit=12 << 20):
    many = isinstance(out_shape, tuple)
    return pl.pallas_call(
        kernel,
        out_shape=out_shape,
        in_specs=in_specs,
        out_specs=(VMEM,) * len(out_shape) if many else VMEM,
        scratch_shapes=scratch,
        compiler_params=pltpu.CompilerParams(vmem_limit_bytes=limit),
    )


def body(long_series, queries, lengths, groups):
    slots, query_len = queries.shape
    rows = long_series.shape[0] // LANES
    chips = lax.axis_size("chip")
    overall = chips * CORES * long_series.shape[0]
    swap = [(0, 1), (1, 0)]
    block = long_series.reshape(rows, LANES)
    gathered = lax.all_to_all(jnp.broadcast_to(block, (chips, rows, LANES)), "chip", 0, 0, tiled=True)
    theirs = lax.ppermute(groups, "core", swap)
    windows, centre, scale = call(
        prepare_queries,
        (
            jax.ShapeDtypeStruct((slots, query_len + LANES, LANES), jnp.bfloat16),
            jax.ShapeDtypeStruct((slots, query_len, LANES), jnp.float32),
            jax.ShapeDtypeStruct((slots, query_len // LANES, LANES), jnp.float32),
        ),
        [VMEM],
    )(queries)
    picked = call(pick, jax.ShapeDtypeStruct(((rows + 8) * slots, LANES), jnp.bfloat16), [SMEM, VMEM])(theirs, gathered)
    passed = lax.ppermute(picked, "core", swap)
    return call(
        functools.partial(join, overall),
        jax.ShapeDtypeStruct((slots, query_len), jnp.float32),
        [SMEM, SMEM, SMEM, VMEM, VMEM, VMEM, VMEM, VMEM],
        [
            pltpu.VMEM((slots, (rows + 5) * LANES, LANES), jnp.bfloat16),
            pltpu.VMEM((2, slots * (rows + 8), LANES), jnp.float32),
            pltpu.VMEM((slots, query_len, LANES), jnp.float32),
            pltpu.VMEM((slots, rows + 8, LANES), jnp.float32),
        ],
    )(lax.axis_index("core").reshape(1), groups, lengths, gathered, passed, windows, centre, scale)


def solution(mesh):
    outer, members = mesh.devices.shape
    pairs = Mesh(mesh.devices.reshape(outer, members // CORES, CORES), ("groups", "chip", "core"))
    every = ("groups", "chip", "core")
    return jax.shard_map(
        body,
        mesh=pairs,
        in_specs=(P(every), P(every, None), P(every), P(every)),
        out_specs=P(every, None),
        check_vma=False,
    )
```

time: 73.8 us -> 59.8 us (0.81)
  the two profiles are of different devices: /device:TPU:514 before, /device:TPU:513 now
where the time goes in v2:
time: 59.8 us; the launch traced here: 59.6 us
  starting transfers between devices  33.7 us (56%)
  Pallas kernels  15.8 us (26%)
  waiting for transfers between devices  7.82 us (13%)
  local copies, waits for them, and re-layouts  2.21 us (4%)
    all_to_all x1, starting transfers between devices, body(): lax.all_to_all(jnp.broadcast_to(block, (chips, rows, LANES)), 'chip', 0,...  21.9 us
    pallas_call x1, Pallas kernels, body(): call(functools.partial(join, overall), jax.ShapeDtypeStruct((slots, query...  14.1 us
    all_to_all x1, waiting for transfers between devices, body(): lax.all_to_all(jnp.broadcast_to(block, (chips, rows, LANES)), 'chip', 0,...  7 us
    ppermute x1, starting transfers between devices, body(): passed = lax.ppermute(picked, 'core', swap)  6.51 us
    ppermute x1, starting transfers between devices, body(): theirs = lax.ppermute(groups, 'core', swap)  5.23 us
    broadcast_in_dim x1, local copies, waits for them, and re-layouts, body(): jnp.broadcast_to(block, (chips, rows, LANES))  1.55 us
  transfers between devices with their start and end apart: 3, of which 2 were waited for; matrix products, arithmetic and copies ran while one was open for 0% of the time, Pallas kernels for 2%

profile of v2, /device:TPU:513, one launch (start us, length us, event | category | flops | bytes accessed | tf_op | source)
XLA Modules:
  0.0 59.6 jit_solution(2114442908109758219)
XLA Ops:
  0.0 1.6 %broadcast_in_dim.3 = bf16[64,32,128]{2,1,0:T(8,128)(2,1)} broadcast(bf16[32,128]{1,0:T(8,128)(2,1)} %bitcast.2), dimensions={1,2} | broadcast | bytes 532480 | tf_op jit(solution)/shard_map/broadcast_in_dim | solution.py:262
  1.6 0.0 copy-start.1
  1.6 21.9 %all-to-all-start = ((bf16[64,32,128]{2,1,0:T(8,128)(2,1)}), bf16[64,32,128]{2,1,0:T(8,128)(2,1)S(1)}, u32[]{:S(2)}, u32[]{:S(2)}) async-start(bf16[64,32,128]{2,1,0:T(8,128)(2,1)} %broadcast_in_dim.3), calls=%async_computation | async-start | bytes 1048576 | tf_op jit(solution)/shard_map/all_to_all | solution.py:262
  23.5 0.0 copy-done.1
  23.5 5.2 %collective-permute-start = (s32[2]{0:T(128)S(1)}, s32[2]{0:T(128)S(1)}, u32[]{:S(2)}, u32[]{:S(2)}) collective-permute-start(s32[2]{0:T(128)S(1)} %copy-done.1), channel_id=1, source_target_pairs={{0,1},{1,0},{2,3},{3,2},{4,5},{5,4},{6,7},{7,6},{8,9},{9,8},{10,11... | collective-permute-start | bytes 32 | tf_op jit(solution)/shard_map/ppermute | solution.py:263
  28.7 0.8 %collective-permute-done.theirs_ref = s32[2]{0:T(128)S(1)} collective-permute-done((s32[2]{0:T(128)S(1)}, s32[2]{0:T(128)S(1)}, u32[]{:S(2)}, u32[]{:S(2)}) %collective-permute-start) | collective-permute-done | bytes 40 | tf_op jit(solution)/shard_map/ppermute | solution.py:263
  29.6 7.0 %all-to-all-done.gathered_ref = bf16[64,32,128]{2,1,0:T(8,128)(2,1)S(1)} async-done(((bf16[64,32,128]{2,1,0:T(8,128)(2,1)}), bf16[64,32,128]{2,1,0:T(8,128)(2,1)S(1)}, u32[]{:S(2)}, u32[]{:S(2)}) %all-to-all-start) | async-done | bytes 524320 | tf_op jit(solution)/shard_map/all_to_all | solution.py:262
  36.6 0.6 shard_map.46
  37.1 0.0 copy-start
  37.1 6.5 %collective-permute-start.1 = (bf16[80,128]{1,0:T(8,128)(2,1)S(1)}, bf16[80,128]{1,0:T(8,128)(2,1)S(1)}, u32[]{:S(2)}, u32[]{:S(2)}) collective-permute-start(bf16[80,128]{1,0:T(8,128)(2,1)S(1)} %shard_map.46), channel_id=1, source_target_pairs={{0,1},{1,0},{2,3},{3,2},{4,5},{5,4},{6,7},{7,6},{8,9},{9,8},{10,11... | collective-permute-start | bytes 61448 | tf_op jit(solution)/shard_map/ppermute | solution.py:274
  43.7 0.0 copy-done
  43.7 1.1 %shard_map.47 = (bf16[2,1152,128]{2,1,0:T(8,128)(2,1)S(1)}, f32[2,1024,128]{2,1,0:T(8,128)S(1)}, f32[2,8,128]{2,1,0:T(8,128)S(1)}) custom-call(bf16[2,1024]{1,0:T(2,128)(2,1)S(1)} %copy-done), custom_call_target="tpu_custom_call" | custom-call | tf_op jit(solution)/shard_map/pallas_call | solution.py:264
  44.8 0.0 collective-permute-done.1.passed_ref
  44.8 0.0 copy-start.2
  44.8 0.6 %copy-done.2 = s32[2]{0:T(128)S(1)} copy-done((s32[2]{0:T(128)S(1)}, s32[2]{0:T(128)}, u32[]{:S(2)}) %copy-start.2) | copy-done | bytes 32
  45.5 14.1 %shard_map.48 = f32[2,1024]{1,0:T(2,128)} custom-call(s32[1]{0:T(128)} %bitcast.core_ref, s32[2]{0:T(128)S(1)} %copy-done.1, s32[2]{0:T(128)S(1)} %copy-done.2, bf16[64,32,128]{2,1,0:T(8,128)(2,1)S(1)} %all-to-all-done.gathered_ref, bf16[80,128]{1,0:T(8,128)(2,1)S(1)} %collective-permute-done.1.passed_ref, ...), custom_call_target="tpu_custom_call" | custom-call | tf_op jit(solution)/shard_map/pallas_call | solution.py:275
Async XLA Ops:
  1.6 21.9 %copy-start.1 = (s32[2]{0:T(128)S(1)}, s32[2]{0:T(128)}, u32[]{:S(2)}) copy-start(s32[2]{0:T(128)} %groups_ref.1) | copy-start | bytes 28
  1.6 35.0 %all-to-all-start = ((bf16[64,32,128]{2,1,0:T(8,128)(2,1)}), bf16[64,32,128]{2,1,0:T(8,128)(2,1)S(1)}, u32[]{:S(2)}, u32[]{:S(2)}) async-start(bf16[64,32,128]{2,1,0:T(8,128)(2,1)} %broadcast_in_dim.3), calls=%async_computation | async-start | bytes 1048576 | tf_op jit(solution)/shard_map/all_to_all | solution.py:262
  23.5 6.0 %collective-permute-start = (s32[2]{0:T(128)S(1)}, s32[2]{0:T(128)S(1)}, u32[]{:S(2)}, u32[]{:S(2)}) collective-permute-start(s32[2]{0:T(128)S(1)} %copy-done.1), channel_id=1, source_target_pairs={{0,1},{1,0},{2,3},{3,2},{4,5},{5,4},{6,7},{7,6},{8,9},{9,8},{10,11... | collective-permute-start | bytes 32 | tf_op jit(solution)/shard_map/ppermute | solution.py:263
  37.1 6.5 %copy-start = (bf16[2,1024]{1,0:T(2,128)(2,1)S(1)}, bf16[2,1024]{1,0:T(2,128)(2,1)}, u32[]{:S(2)}) copy-start(bf16[2,1024]{1,0:T(2,128)(2,1)} %queries_ref.1) | copy-start | bytes 12292
  37.1 7.7 %collective-permute-start.1 = (bf16[80,128]{1,0:T(8,128)(2,1)S(1)}, bf16[80,128]{1,0:T(8,128)(2,1)S(1)}, u32[]{:S(2)}, u32[]{:S(2)}) collective-permute-start(bf16[80,128]{1,0:T(8,128)(2,1)S(1)} %shard_map.46), channel_id=1, source_target_pairs={{0,1},{1,0},{2,3},{3,2},{4,5},{5,4},{6,7},{7,6},{8,9},{9,8},{10,11... | collective-permute-start | bytes 61448 | tf_op jit(solution)/shard_map/ppermute | solution.py:274
  44.8 0.7 %copy-start.2 = (s32[2]{0:T(128)S(1)}, s32[2]{0:T(128)}, u32[]{:S(2)}) copy-start(s32[2]{0:T(128)} %lengths_ref.1) | copy-start | bytes 28

commit v3 on v2

v3 whole, which is shorter than its diff:
```python
import functools

import jax
import jax.numpy as jnp
from jax import lax
from jax.experimental import pallas as pl
from jax.experimental.pallas import tpu as pltpu
from jax.sharding import Mesh
from jax.sharding import PartitionSpec as P


M = 256
LANES = 128
SPREAD_FLOOR = 0.25
CORES = 2
NEVER = -3.0e38
PIECE = 64
LAG = 8


def lane_iota(rows):
    return lax.broadcasted_iota(jnp.int32, (rows, LANES), 1)


def ahead(x, n, width):
    rows = x.shape[0]
    below = pltpu.roll(x, rows - 1, axis=0)
    if n == width:
        return below
    lane = lane_iota(rows)
    return jnp.where(lane < width - n, pltpu.roll(x, width - n, axis=1), pltpu.roll(below, width - n, axis=1))


def window_stats(x):
    total = x
    squares = jnp.zeros_like(x)
    n = 1
    while n < M:
        other = ahead(total, n, LANES)
        apart = total - other
        squares = squares + apart * apart * (0.5 / n)
        if n > 1:
            squares = squares + ahead(merged, n, LANES)
        merged = squares
        total = total + other
        n *= 2
    centre = total * (1.0 / M)
    spread = jnp.sqrt(squares * (1.0 / M) + SPREAD_FLOOR)
    return centre, spread


def sheared(row, shift):
    return pltpu.roll(jnp.broadcast_to(row, (LANES, LANES)), shift, axis=1, stride=1, stride_axis=0)


def prepare_queries(lengths_ref, queries_ref, turned_ref, windows_ref, centre_ref, ends_ref):
    count, length = queries_ref.shape
    rows = length // LANES
    zero = jnp.zeros((1, LANES), jnp.float32)
    upper = lane_iota(LANES) >= lax.broadcasted_iota(jnp.int32, (LANES, LANES), 0)
    place = LANES * lax.broadcasted_iota(jnp.int32, (rows, LANES), 0) + lane_iota(rows)
    for s in range(count):
        parts = [
            queries_ref[s : s + 1, LANES * b : LANES * (b + 1)].astype(jnp.float32)
            for b in range(rows)
        ]
        turned = [turned_ref[s : s + 1, length - LANES * (b + 1) : length - LANES * b] for b in range(rows)]
        turned = [sheared(row.astype(jnp.float32), 0) for row in turned] + [jnp.zeros((LANES, LANES), jnp.float32)] * 2
        for b in range(rows + 1):
            tile = jnp.where(upper, turned[b], turned[b + 1])
            windows_ref[s, LANES * b : LANES * (b + 1), :] = tile.astype(jnp.bfloat16)
        series = jnp.concatenate(parts + [zero] * 8, axis=0)
        centre, spread = window_stats(series)
        live = place <= lengths_ref[s] - M
        ends_ref[0, s] = jnp.where(live, 2.0, 0.0)
        ends_ref[1, s] = jnp.where(live, 2.0 / (M * spread[:rows]), 0.0)
        for b in range(rows):
            wide = jnp.broadcast_to(centre[b : b + 1], (LANES, LANES))
            centre_ref[s, LANES * b : LANES * (b + 1), :] = wide.T


def pick(theirs_ref, gathered_ref, out_ref):
    held, rows, _ = gathered_ref.shape
    slots = theirs_ref.shape[0]
    for s in range(slots):
        want = theirs_ref[s]
        out_ref[rows * s : rows * (s + 1), :] = gathered_ref[want // CORES]
        follow = jnp.minimum((want + 1) // CORES, held - 1)
        out_ref[rows * slots + 8 * s : rows * slots + 8 * (s + 1), :] = gathered_ref[follow, 0:8, :]


def join(overall, core_ref, groups_ref, gathered_ref, passed_ref, windows_ref, centre_ref, ends_ref, out_ref, ref_windows, weights, running, series):
    held, rows, _ = gathered_ref.shape
    slots = groups_ref.shape[0]
    block_len = rows * LANES
    query_len = centre_ref.shape[1]
    tail = rows - M // LANES
    parts = []
    for s in range(slots):
        region = groups_ref[s]
        follow = jnp.minimum((region + 1) // CORES, held - 1)
        block = jnp.where(
            lax.rem(region, CORES) == core_ref[0],
            gathered_ref[region // CORES].astype(jnp.float32),
            passed_ref[rows * s : rows * (s + 1), :].astype(jnp.float32),
        )
        halo = jnp.where(
            lax.rem(region + 1, CORES) == core_ref[0],
            gathered_ref[follow, 0:8, :].astype(jnp.float32),
            passed_ref[rows * slots + 8 * s : rows * slots + 8 * (s + 1), :].astype(jnp.float32),
        )
        parts.append(jnp.concatenate([block, halo], axis=0))
    every = jnp.concatenate(parts, axis=0)
    later = ahead(every, 1, LANES)
    centre, spread = window_stats(every)
    inverse = 1.0 / spread
    factors = [inverse, (M * centre) * inverse]
    for s in range(slots):
        first = (rows + 8) * s
        ends = groups_ref[s] * block_len + block_len > overall - M

        def moved(x, x_later, count):
            early = x_later[first + tail - 2 : first + tail - 2 + count]
            return jnp.where(ends, early, x[first + tail : first + tail + count])

        series[s, :rows, :] = every[first : first + rows]
        series[s, rows : rows + 4, :] = moved(every, later, 4)
        for w in range(2):
            weights[w, first : first + tail, :] = factors[w][first : first + tail]
            weights[w, first + tail : first + rows, :] = moved(factors[w], ahead(factors[w], 1, LANES), 2)
    trips = block_len // (2 * M)
    lines = (rows + 2) * LANES
    pieces = query_len // PIECE

    def compute(*accs):
        def push(u):
            s, t = u // trips, u % trips
            for q in range(2):
                j = lines - M - 2 * M * t - M * q
                if q:
                    j = j - jnp.where(t == trips - 1, LANES, 0)
                tile = [ref_windows[s, pl.ds(pl.multiple_of(j - LANES * h, LANES), M), :] for h in range(2)]
                pltpu.matmul_push_rhs(jnp.concatenate(tile, axis=1), staging_register=0, mxu_index=q)

        def rows_at(u):
            top = (rows + 8) * (u // trips) + 4 * (u % trips)
            return [
                [jnp.broadcast_to(weights[w, pl.ds(top + k, 1), :], (8, LANES)) for k in range(4)] for w in range(2)
            ]

        def drain(u, n, scale, shift):
            s = u // trips
            both = [pltpu.matmul_pop(accs[2 * n + q]) for q in range(2)]
            for r in range(0, PIECE, 8):
                at = PIECE * n + r
                mean = centre_ref[s, at : at + 8, :]
                found = [
                    both[k // 2][r : r + 8, LANES * (k % 2) : LANES * (k % 2 + 1)] * scale[k] - mean * shift[k]
                    for k in range(4)
                ]
                best = jnp.maximum(jnp.maximum(found[0], found[1]), jnp.maximum(found[2], found[3]))
                running[s, at : at + 8, :] = jnp.maximum(running[s, at : at + 8, :], best)

        def trip(u, first, last):
            s = u // trips
            before = None if first else rows_at(u - 1)
            now = rows_at(u)
            for n in range(pieces):
                i = PIECE * n
                lhs = jnp.concatenate(
                    [windows_ref[s, i + LANES : i + LANES + PIECE, :], windows_ref[s, i : i + PIECE, :]], axis=1
                )
                if n >= LAG:
                    drain(u, n - LAG, *now)
                elif not first:
                    drain(u - 1, pieces + n - LAG, *before)
                for q in range(2):
                    pltpu.matmul_acc_lhs(accs[2 * n + q], lhs, load_staged_rhs=0 if n == 0 else None)
                if n == 0 and not last:
                    push(u + 1)
            if last:
                for n in range(pieces - LAG, pieces):
                    drain(u, n, *now)

        for acc in accs:
            pltpu.matmul_pop(acc)
        push(0)
        trip(0, True, False)

        def middle(u, carry):
            trip(u, False, False)
            return carry

        lax.fori_loop(1, slots * trips - 1, middle, 0)
        trip(slots * trips - 1, False, True)

    running[...] = jnp.full(running.shape, NEVER, jnp.float32)
    lower = lane_iota(LANES) <= lax.broadcasted_iota(jnp.int32, (LANES, LANES), 0)
    own = [None] * slots
    for b in range(rows + 4):
        for s in range(slots):
            after = sheared(series[s, b : b + 1, :], 1)
            if b not in (0, rows):
                at = lines - LANES * (b - b // rows)
                ref_windows[s, at : at + LANES, :] = jnp.where(lower, own[s], after).astype(jnp.bfloat16)
            own[s] = after

    pl.run_scoped(
        compute,
        *[pltpu.ACC(n % 2)((PIECE, 2 * LANES), jnp.float32) for n in range(2 * pieces)],
    )
    for s in range(slots):
        for b in range(query_len // LANES):
            best = jnp.max(running[s, LANES * b : LANES * (b + 1), :].T, axis=0, keepdims=True)
            out_ref[s : s + 1, LANES * b : LANES * (b + 1)] = (
                ends_ref[0, s, b : b + 1, :] - best * ends_ref[1, s, b : b + 1, :]
            )


VMEM = pl.BlockSpec(memory_space=pltpu.VMEM)
SMEM = pl.BlockSpec(memory_space=pltpu.SMEM)


def call(kernel, out_shape, in_specs, scratch=(), limit=12 << 20):
    many = isinstance(out_shape, tuple)
    return pl.pallas_call(
        kernel,
        out_shape=out_shape,
        in_specs=in_specs,
        out_specs=(VMEM,) * len(out_shape) if many else VMEM,
        scratch_shapes=scratch,
        compiler_params=pltpu.CompilerParams(vmem_limit_bytes=limit),
    )


def prepare_call(slots, query_len):
    return call(
        prepare_queries,
        (
            jax.ShapeDtypeStruct((slots, query_len + LANES, LANES), jnp.bfloat16),
            jax.ShapeDtypeStruct((slots, query_len, LANES), jnp.float32),
            jax.ShapeDtypeStruct((2, slots, query_len // LANES, LANES), jnp.float32),
        ),
        [SMEM, VMEM, VMEM],
    )


def join_call(slots, rows, query_len, overall):
    return call(
        functools.partial(join, overall),
        jax.ShapeDtypeStruct((slots, query_len), jnp.float32),
        [SMEM, SMEM, VMEM, VMEM, VMEM, VMEM, VMEM],
        [
            pltpu.VMEM((slots, (rows + 2) * LANES, LANES), jnp.bfloat16),
            pltpu.VMEM((2, slots * (rows + 8), LANES), jnp.float32),
            pltpu.VMEM((slots, query_len, LANES), jnp.float32),
            pltpu.VMEM((slots, rows + 8, LANES), jnp.float32),
        ],
    )


def body(long_series, queries, lengths, groups):
    slots, query_len = queries.shape
    rows = long_series.shape[0] // LANES
    chips = lax.axis_size("chip")
    overall = chips * CORES * long_series.shape[0]
    swap = [(0, 1), (1, 0)]
    block = long_series.reshape(rows, LANES)
    gathered = lax.all_to_all(jnp.broadcast_to(block, (chips, rows, LANES)), "chip", 0, 0, tiled=True)
    theirs = lax.ppermute(groups, "core", swap)
    windows, centre, ends = prepare_call(slots, query_len)(lengths, queries, queries[:, ::-1])
    picked = call(pick, jax.ShapeDtypeStruct(((rows + 8) * slots, LANES), jnp.bfloat16), [SMEM, VMEM])(theirs, gathered)
    passed = lax.ppermute(picked, "core", swap)
    core = lax.axis_index("core").reshape(1)
    return join_call(slots, rows, query_len, overall)(core, groups, gathered, passed, windows, centre, ends)


def solution(mesh):
    outer, members = mesh.devices.shape
    pairs = Mesh(mesh.devices.reshape(outer, members // CORES, CORES), ("groups", "chip", "core"))
    every = ("groups", "chip", "core")
    return jax.shard_map(
        body,
        mesh=pairs,
        in_specs=(P(every), P(every, None), P(every), P(every)),
        out_specs=P(every, None),
        check_vma=False,
    )
```

time: 59.8 us -> 54.9 us (0.918)
  Pallas kernels: 15.8 us -> 10.8 us
    pallas_call x2, Pallas kernels: 15.2 us -> 10.2 us  [the longest x1 8.71 us: body(): join_call(slots, rows, query_len, overall)]
    rev x0 -> x1, local copies, waits for them, and re-layouts: none -> 0.72 us  [body(): queries[:, ::-1]]
    unnamed x6, local copies, waits for them, and re-layouts: 0.66 us -> 0.01 us
  transfers between devices with their start and end apart: 3 -> 3, of which waited for: 2 -> 2; matrix products, arithmetic and copies ran while one was open for 0% -> 1% of each run, Pallas kernels for 2% -> 3%
where the time goes in v3:
time: 54.9 us; the launch traced here: 54.6 us
  starting transfers between devices  33.7 us (61%)
  Pallas kernels  10.8 us (20%)
  waiting for transfers between devices  7.82 us (14%)
  local copies, waits for them, and re-layouts  2.29 us (4%)
    all_to_all x1, starting transfers between devices, body(): lax.all_to_all(jnp.broadcast_to(block, (chips, rows, LANES)), 'chip', 0,...  21.9 us
    pallas_call x1, Pallas kernels, body(): join_call(slots, rows, query_len, overall)  8.71 us
    all_to_all x1, waiting for transfers between devices, body(): lax.all_to_all(jnp.broadcast_to(block, (chips, rows, LANES)), 'chip', 0,...  7 us
    ppermute x1, starting transfers between devices, body(): passed = lax.ppermute(picked, 'core', swap)  6.51 us
    ppermute x1, starting transfers between devices, body(): theirs = lax.ppermute(groups, 'core', swap)  5.23 us
    broadcast_in_dim x1, local copies, waits for them, and re-layouts, body(): jnp.broadcast_to(block, (chips, rows, LANES))  1.55 us
    pallas_call x1, Pallas kernels, body(): prepare_call(slots, query_len)(lengths, queries, queries[:, ::-1])  1.54 us
  transfers between devices with their start and end apart: 3, of which 2 were waited for; matrix products, arithmetic and copies ran while one was open for 1% of the time, Pallas kernels for 3%

profile of v3, /device:TPU:513, one launch (start us, length us, event | category | flops | bytes accessed | tf_op | source)
XLA Modules:
  0.0 54.6 jit_solution(6035319631123499122)
XLA Ops:
  0.0 1.6 %broadcast_in_dim.3 = bf16[64,32,128]{2,1,0:T(8,128)(2,1)} broadcast(bf16[32,128]{1,0:T(8,128)(2,1)} %bitcast.2), dimensions={1,2} | broadcast | bytes 532480 | tf_op jit(solution)/shard_map/broadcast_in_dim | solution.py:269
  1.6 0.0 copy-start.2
  1.6 21.9 %all-to-all-start = ((bf16[64,32,128]{2,1,0:T(8,128)(2,1)}), bf16[64,32,128]{2,1,0:T(8,128)(2,1)S(1)}, u32[]{:S(2)}, u32[]{:S(2)}) async-start(bf16[64,32,128]{2,1,0:T(8,128)(2,1)} %broadcast_in_dim.3), calls=%async_computation | async-start | bytes 1048576 | tf_op jit(solution)/shard_map/all_to_all | solution.py:269
  23.5 0.0 copy-done.2
  23.5 5.2 %collective-permute-start = (s32[2]{0:T(128)S(1)}, s32[2]{0:T(128)S(1)}, u32[]{:S(2)}, u32[]{:S(2)}) collective-permute-start(s32[2]{0:T(128)S(1)} %copy-done.2), channel_id=1, source_target_pairs={{0,1},{1,0},{2,3},{3,2},{4,5},{5,4},{6,7},{7,6},{8,9},{9,8},{10,11... | collective-permute-start | bytes 32 | tf_op jit(solution)/shard_map/ppermute | solution.py:270
  28.7 0.8 %collective-permute-done.theirs_ref = s32[2]{0:T(128)S(1)} collective-permute-done((s32[2]{0:T(128)S(1)}, s32[2]{0:T(128)S(1)}, u32[]{:S(2)}, u32[]{:S(2)}) %collective-permute-start) | collective-permute-done | bytes 40 | tf_op jit(solution)/shard_map/ppermute | solution.py:270
  29.6 7.0 %all-to-all-done.gathered_ref = bf16[64,32,128]{2,1,0:T(8,128)(2,1)S(1)} async-done(((bf16[64,32,128]{2,1,0:T(8,128)(2,1)}), bf16[64,32,128]{2,1,0:T(8,128)(2,1)S(1)}, u32[]{:S(2)}, u32[]{:S(2)}) %all-to-all-start) | async-done | bytes 524320 | tf_op jit(solution)/shard_map/all_to_all | solution.py:269
  36.6 0.6 %shard_map.46 = bf16[80,128]{1,0:T(8,128)(2,1)S(1)} custom-call(s32[2]{0:T(128)S(1)} %collective-permute-done.theirs_ref, bf16[64,32,128]{2,1,0:T(8,128)(2,1)S(1)} %all-to-all-done.gathered_ref), custom_call_target="tpu_custom_call" | custom-call | tf_op jit(solution)/shard_map/pallas_call | solution.py:272
  37.1 0.0 copy-start
  37.1 6.5 %collective-permute-start.1 = (bf16[80,128]{1,0:T(8,128)(2,1)S(1)}, bf16[80,128]{1,0:T(8,128)(2,1)S(1)}, u32[]{:S(2)}, u32[]{:S(2)}) collective-permute-start(bf16[80,128]{1,0:T(8,128)(2,1)S(1)} %shard_map.46), channel_id=1, source_target_pairs={{0,1},{1,0},{2,3},{3,2},{4,5},{5,4},{6,7},{7,6},{8,9},{9,8},{10,11... | collective-permute-start | bytes 61448 | tf_op jit(solution)/shard_map/ppermute | solution.py:273
  43.7 0.0 copy-done
  43.7 0.0 copy-start.1
  43.7 0.7 %rev.3.turned_ref = bf16[2,1024]{1,0:T(2,128)(2,1)S(1)} reverse(bf16[2,1024]{1,0:T(2,128)(2,1)S(1)} %copy-done), dimensions={1} | reverse | bytes 8192 | tf_op jit(solution)/shard_map/rev | solution.py:271
  44.4 0.0 copy-done.1
  44.4 1.5 %shard_map.47 = (bf16[2,1152,128]{2,1,0:T(8,128)(2,1)S(1)}, f32[2,1024,128]{2,1,0:T(8,128)S(1)}, f32[2,2,8,128]{3,2,1,0:T(8,128)S(1)}) custom-call(s32[2]{0:T(128)S(1)} %copy-done.1, bf16[2,1024]{1,0:T(2,128)(2,1)S(1)} %copy-done, bf16[2,1024]{1,0:T(2,128)(2,1)S(1)} %rev.3.turned_ref), custom_call_target="tpu_custom_call" | custom-call | tf_op jit(solution)/shard_map/pallas_call | solution.py:271
  45.9 0.0 collective-permute-done.1.passed_ref
  45.9 8.7 %shard_map.48 = f32[2,1024]{1,0:T(2,128)} custom-call(s32[1]{0:T(128)} %bitcast.core_ref, s32[2]{0:T(128)S(1)} %copy-done.2, bf16[64,32,128]{2,1,0:T(8,128)(2,1)S(1)} %all-to-all-done.gathered_ref, bf16[80,128]{1,0:T(8,128)(2,1)S(1)} %collective-permute-done.1.passed_ref, bf16[2,1152,128]{2,1,0:T(8,128)(2,1)S(1)} %get-tuple-element.8.windows_ref, ...), custom_call_target="tpu_custom_call" | custom-call | tf_op jit(solution)/shard_map/pallas_call | solution.py:275
Async XLA Ops:
  1.6 21.9 %copy-start.2 = (s32[2]{0:T(128)S(1)}, s32[2]{0:T(128)}, u32[]{:S(2)}) copy-start(s32[2]{0:T(128)} %groups_ref.1) | copy-start | bytes 28
  1.6 35.0 %all-to-all-start = ((bf16[64,32,128]{2,1,0:T(8,128)(2,1)}), bf16[64,32,128]{2,1,0:T(8,128)(2,1)S(1)}, u32[]{:S(2)}, u32[]{:S(2)}) async-start(bf16[64,32,128]{2,1,0:T(8,128)(2,1)} %broadcast_in_dim.3), calls=%async_computation | async-start | bytes 1048576 | tf_op jit(solution)/shard_map/all_to_all | solution.py:269
  23.5 6.0 %collective-permute-start = (s32[2]{0:T(128)S(1)}, s32[2]{0:T(128)S(1)}, u32[]{:S(2)}, u32[]{:S(2)}) collective-permute-start(s32[2]{0:T(128)S(1)} %copy-done.2), channel_id=1, source_target_pairs={{0,1},{1,0},{2,3},{3,2},{4,5},{5,4},{6,7},{7,6},{8,9},{9,8},{10,11... | collective-permute-start | bytes 32 | tf_op jit(solution)/shard_map/ppermute | solution.py:270
  37.1 6.5 %copy-start = (bf16[2,1024]{1,0:T(2,128)(2,1)S(1)}, bf16[2,1024]{1,0:T(2,128)(2,1)}, u32[]{:S(2)}) copy-start(bf16[2,1024]{1,0:T(2,128)(2,1)} %queries_ref.1) | copy-start | bytes 12292
  37.1 8.8 %collective-permute-start.1 = (bf16[80,128]{1,0:T(8,128)(2,1)S(1)}, bf16[80,128]{1,0:T(8,128)(2,1)S(1)}, u32[]{:S(2)}, u32[]{:S(2)}) collective-permute-start(bf16[80,128]{1,0:T(8,128)(2,1)S(1)} %shard_map.46), channel_id=1, source_target_pairs={{0,1},{1,0},{2,3},{3,2},{4,5},{5,4},{6,7},{7,6},{8,9},{9,8},{10,11... | collective-permute-start | bytes 61448 | tf_op jit(solution)/shard_map/ppermute | solution.py:273
  43.7 0.7 %copy-start.1 = (s32[2]{0:T(128)S(1)}, s32[2]{0:T(128)}, u32[]{:S(2)}) copy-start(s32[2]{0:T(128)} %lengths_ref.1) | copy-start | bytes 28

commit v4 on v3

--- a/solution.py
+++ b/solution.py
@@ -14,36 +14,37 @@
 SPREAD_FLOOR = 0.25
 CORES = 2
 NEVER = -3.0e38
-PIECE = 64
-LAG = 8
+PIECE = 128
+LAG = 3
 
 
 def lane_iota(rows):
     return lax.broadcasted_iota(jnp.int32, (rows, LANES), 1)
 
 
-def ahead(x, n, width):
+def ahead(x, n):
     rows = x.shape[0]
-    below = pltpu.roll(x, rows - 1, axis=0)
-    if n == width:
-        return below
-    lane = lane_iota(rows)
-    return jnp.where(lane < width - n, pltpu.roll(x, width - n, axis=1), pltpu.roll(below, width - n, axis=1))
+    if n % LANES == 0:
+        return pltpu.roll(x, rows - n // LANES, axis=0)
+    turned = pltpu.roll(x, LANES - n % LANES, axis=1)
+    below = pltpu.roll(turned, rows - n // LANES - 1, axis=0)
+    if n >= LANES:
+        turned = pltpu.roll(turned, rows - n // LANES, axis=0)
+    return jnp.where(lane_iota(rows) < LANES - n % LANES, turned, below)
 
 
 def window_stats(x):
-    total = x
-    squares = jnp.zeros_like(x)
-    n = 1
+    total, squares, n = x, None, 1
     while n < M:
-        other = ahead(total, n, LANES)
-        apart = total - other
-        squares = squares + apart * apart * (0.5 / n)
+        sums = [total] + [ahead(total, n * k) for k in range(1, 4)]
+        whole = (sums[0] + sums[1]) + (sums[2] + sums[3])
+        apart = [(piece - whole * 0.25) for piece in sums]
+        spare = ((apart[0] * apart[0] + apart[1] * apart[1]) + (apart[2] * apart[2] + apart[3] * apart[3])) * (1.0 / n)
         if n > 1:
-            squares = squares + ahead(merged, n, LANES)
-        merged = squares
-        total = total + other
-        n *= 2
+            kept = [squares] + [ahead(squares, n * k) for k in range(1, 4)]
+            spare = spare + ((kept[0] + kept[1]) + (kept[2] + kept[3]))
+        total, squares = whole, spare
+        n *= 4
     centre = total * (1.0 / M)
     spread = jnp.sqrt(squares * (1.0 / M) + SPREAD_FLOOR)
     return centre, spread
@@ -111,7 +112,7 @@
         )
         parts.append(jnp.concatenate([block, halo], axis=0))
     every = jnp.concatenate(parts, axis=0)
-    later = ahead(every, 1, LANES)
+    later = ahead(every, 1)
     centre, spread = window_stats(every)
     inverse = 1.0 / spread
     factors = [inverse, (M * centre) * inverse]
@@ -127,7 +128,23 @@
         series[s, rows : rows + 4, :] = moved(every, later, 4)
         for w in range(2):
             weights[w, first : first + tail, :] = factors[w][first : first + tail]
-            weights[w, first + tail : first + rows, :] = moved(factors[w], ahead(factors[w], 1, LANES), 2)
+            weights[w, first + tail : first + rows, :] = moved(factors[w], ahead(factors[w], 1), 2)
+    lower = lane_iota(LANES) <= lax.broadcasted_iota(jnp.int32, (LANES, LANES), 0)
+    own = [None] * slots
+
+    def build(s, b):
+        after = sheared(series[s, b : b + 1, :], 1)
+        if b not in (0, rows):
+            at = lines - LANES * (b - b // rows)
+            ref_windows[s, at : at + LANES, :] = jnp.where(lower, own[s], after).astype(jnp.bfloat16)
+        own[s] = after
+
+    def finish(s, b):
+        best = jnp.max(running[s, LANES * b : LANES * (b + 1), :].T, axis=0, keepdims=True)
+        out_ref[s : s + 1, LANES * b : LANES * (b + 1)] = (
+            ends_ref[0, s, b : b + 1, :] - best * ends_ref[1, s, b : b + 1, :]
+        )
+
     trips = block_len // (2 * M)
     lines = (rows + 2) * LANES
     pieces = query_len // PIECE
@@ -161,8 +178,10 @@
                 best = jnp.maximum(jnp.maximum(found[0], found[1]), jnp.maximum(found[2], found[3]))
                 running[s, at : at + 8, :] = jnp.maximum(running[s, at : at + 8, :], best)
 
-        def trip(u, first, last):
+        def trip(u, first, last, extras=()):
             s = u // trips
+            extras = list(extras)
+            share = -(-len(extras) // pieces)
             before = None if first else rows_at(u - 1)
             now = rows_at(u)
             for n in range(pieces):
@@ -176,7 +195,9 @@
                     drain(u - 1, pieces + n - LAG, *before)
                 for q in range(2):
                     pltpu.matmul_acc_lhs(accs[2 * n + q], lhs, load_staged_rhs=0 if n == 0 else None)
-                if n == 0 and not last:
+                for extra in extras[share * n : share * (n + 1)]:
+                    extra()
+                if n == (pieces - 2 if first else 0) and not last:
                     push(u + 1)
             if last:
                 for n in range(pieces - LAG, pieces):
@@ -184,37 +205,28 @@
 
         for acc in accs:
             pltpu.matmul_pop(acc)
+        order = [(s, b) for s in range(slots) for b in range(rows + 4)]
+        early = 2 * M // LANES + 2
+        for s, b in order[:early]:
+            build(s, b)
         push(0)
-        trip(0, True, False)
+        trip(0, True, False, [functools.partial(build, s, b) for s, b in order[early:]])
 
         def middle(u, carry):
             trip(u, False, False)
             return carry
 
         lax.fori_loop(1, slots * trips - 1, middle, 0)
-        trip(slots * trips - 1, False, True)
+        done = [(s, b) for s in range(slots - 1) for b in range(query_len // LANES)]
+        trip(slots * trips - 1, False, True, [functools.partial(finish, s, b) for s, b in done])
+        for b in range(query_len // LANES):
+            finish(slots - 1, b)
 
     running[...] = jnp.full(running.shape, NEVER, jnp.float32)
-    lower = lane_iota(LANES) <= lax.broadcasted_iota(jnp.int32, (LANES, LANES), 0)
-    own = [None] * slots
-    for b in range(rows + 4):
-        for s in range(slots):
-            after = sheared(series[s, b : b + 1, :], 1)
-            if b not in (0, rows):
-                at = lines - LANES * (b - b // rows)
-                ref_windows[s, at : at + LANES, :] = jnp.where(lower, own[s], after).astype(jnp.bfloat16)
-            own[s] = after
-
     pl.run_scoped(
         compute,
         *[pltpu.ACC(n % 2)((PIECE, 2 * LANES), jnp.float32) for n in range(2 * pieces)],
     )
-    for s in range(slots):
-        for b in range(query_len // LANES):
-            best = jnp.max(running[s, LANES * b : LANES * (b + 1), :].T, axis=0, keepdims=True)
-            out_ref[s : s + 1, LANES * b : LANES * (b + 1)] = (
-                ends_ref[0, s, b : b + 1, :] - best * ends_ref[1, s, b : b + 1, :]
-            )
 
 
 VMEM = pl.BlockSpec(memory_space=pltpu.VMEM)

time: 54.9 us -> 54.3 us (0.989)
  Pallas kernels: 10.8 us -> 10.2 us
where the time goes in v4:
time: 54.3 us; the launch traced here: 54 us
  starting transfers between devices  33.7 us (62%)
  Pallas kernels  10.2 us (19%)
  waiting for transfers between devices  7.82 us (14%)
  local copies, waits for them, and re-layouts  2.29 us (4%)
    all_to_all x1, starting transfers between devices, body(): lax.all_to_all(jnp.broadcast_to(block, (chips, rows, LANES)), 'chip', 0,...  21.9 us
    pallas_call x1, Pallas kernels, body(): join_call(slots, rows, query_len, overall)  8.23 us
    all_to_all x1, waiting for transfers between devices, body(): lax.all_to_all(jnp.broadcast_to(block, (chips, rows, LANES)), 'chip', 0,...  7 us
    ppermute x1, starting transfers between devices, body(): passed = lax.ppermute(picked, 'core', swap)  6.51 us
    ppermute x1, starting transfers between devices, body(): theirs = lax.ppermute(groups, 'core', swap)  5.23 us
    broadcast_in_dim x1, local copies, waits for them, and re-layouts, body(): jnp.broadcast_to(block, (chips, rows, LANES))  1.55 us
    pallas_call x1, Pallas kernels, body(): prepare_call(slots, query_len)(lengths, queries, queries[:, ::-1])  1.38 us
  transfers between devices with their start and end apart: 3, of which 2 were waited for; matrix products, arithmetic and copies ran while one was open for 1% of the time, Pallas kernels for 3%

profile of v4, /device:TPU:513, one launch (start us, length us, event | category | flops | bytes accessed | tf_op | source)
XLA Modules:
  0.0 54.0 jit_solution(6825500448581622437)
XLA Ops:
  0.0 1.6 %broadcast_in_dim.3 = bf16[64,32,128]{2,1,0:T(8,128)(2,1)} broadcast(bf16[32,128]{1,0:T(8,128)(2,1)} %bitcast.2), dimensions={1,2} | broadcast | bytes 532480 | tf_op jit(solution)/shard_map/broadcast_in_dim | solution.py:281
  1.6 0.0 copy-start.2
  1.6 21.9 %all-to-all-start = ((bf16[64,32,128]{2,1,0:T(8,128)(2,1)}), bf16[64,32,128]{2,1,0:T(8,128)(2,1)S(1)}, u32[]{:S(2)}, u32[]{:S(2)}) async-start(bf16[64,32,128]{2,1,0:T(8,128)(2,1)} %broadcast_in_dim.3), calls=%async_computation | async-start | bytes 1048576 | tf_op jit(solution)/shard_map/all_to_all | solution.py:281
  23.5 0.0 copy-done.2
  23.5 5.2 %collective-permute-start = (s32[2]{0:T(128)S(1)}, s32[2]{0:T(128)S(1)}, u32[]{:S(2)}, u32[]{:S(2)}) collective-permute-start(s32[2]{0:T(128)S(1)} %copy-done.2), channel_id=1, source_target_pairs={{0,1},{1,0},{2,3},{3,2},{4,5},{5,4},{6,7},{7,6},{8,9},{9,8},{10,11... | collective-permute-start | bytes 32 | tf_op jit(solution)/shard_map/ppermute | solution.py:282
  28.7 0.8 %collective-permute-done.theirs_ref = s32[2]{0:T(128)S(1)} collective-permute-done((s32[2]{0:T(128)S(1)}, s32[2]{0:T(128)S(1)}, u32[]{:S(2)}, u32[]{:S(2)}) %collective-permute-start) | collective-permute-done | bytes 40 | tf_op jit(solution)/shard_map/ppermute | solution.py:282
  29.6 7.0 %all-to-all-done.gathered_ref = bf16[64,32,128]{2,1,0:T(8,128)(2,1)S(1)} async-done(((bf16[64,32,128]{2,1,0:T(8,128)(2,1)}), bf16[64,32,128]{2,1,0:T(8,128)(2,1)S(1)}, u32[]{:S(2)}, u32[]{:S(2)}) %all-to-all-start) | async-done | bytes 524320 | tf_op jit(solution)/shard_map/all_to_all | solution.py:281
  36.6 0.6 %shard_map.46 = bf16[80,128]{1,0:T(8,128)(2,1)S(1)} custom-call(s32[2]{0:T(128)S(1)} %collective-permute-done.theirs_ref, bf16[64,32,128]{2,1,0:T(8,128)(2,1)S(1)} %all-to-all-done.gathered_ref), custom_call_target="tpu_custom_call" | custom-call | tf_op jit(solution)/shard_map/pallas_call | solution.py:284
  37.1 0.0 copy-start
  37.1 6.5 %collective-permute-start.1 = (bf16[80,128]{1,0:T(8,128)(2,1)S(1)}, bf16[80,128]{1,0:T(8,128)(2,1)S(1)}, u32[]{:S(2)}, u32[]{:S(2)}) collective-permute-start(bf16[80,128]{1,0:T(8,128)(2,1)S(1)} %shard_map.46), channel_id=1, source_target_pairs={{0,1},{1,0},{2,3},{3,2},{4,5},{5,4},{6,7},{7,6},{8,9},{9,8},{10,11... | collective-permute-start | bytes 61448 | tf_op jit(solution)/shard_map/ppermute | solution.py:285
  43.7 0.0 copy-done
  43.7 0.0 copy-start.1
  43.7 0.7 %rev.3.turned_ref = bf16[2,1024]{1,0:T(2,128)(2,1)S(1)} reverse(bf16[2,1024]{1,0:T(2,128)(2,1)S(1)} %copy-done), dimensions={1} | reverse | bytes 8192 | tf_op jit(solution)/shard_map/rev | solution.py:283
  44.4 0.0 copy-done.1
  44.4 1.4 %shard_map.47 = (bf16[2,1152,128]{2,1,0:T(8,128)(2,1)S(1)}, f32[2,1024,128]{2,1,0:T(8,128)S(1)}, f32[2,2,8,128]{3,2,1,0:T(8,128)S(1)}) custom-call(s32[2]{0:T(128)S(1)} %copy-done.1, bf16[2,1024]{1,0:T(2,128)(2,1)S(1)} %copy-done, bf16[2,1024]{1,0:T(2,128)(2,1)S(1)} %rev.3.turned_ref), custom_call_target="tpu_custom_call" | custom-call | tf_op jit(solution)/shard_map/pallas_call | solution.py:283
  45.8 0.0 collective-permute-done.1.passed_ref
  45.8 8.2 %shard_map.48 = f32[2,1024]{1,0:T(2,128)} custom-call(s32[1]{0:T(128)} %bitcast.core_ref, s32[2]{0:T(128)S(1)} %copy-done.2, bf16[64,32,128]{2,1,0:T(8,128)(2,1)S(1)} %all-to-all-done.gathered_ref, bf16[80,128]{1,0:T(8,128)(2,1)S(1)} %collective-permute-done.1.passed_ref, bf16[2,1152,128]{2,1,0:T(8,128)(2,1)S(1)} %get-tuple-element.8.windows_ref, ...), custom_call_target="tpu_custom_call" | custom-call | tf_op jit(solution)/shard_map/pallas_call | solution.py:287
Async XLA Ops:
  1.6 21.9 %copy-start.2 = (s32[2]{0:T(128)S(1)}, s32[2]{0:T(128)}, u32[]{:S(2)}) copy-start(s32[2]{0:T(128)} %groups_ref.1) | copy-start | bytes 28
  1.6 35.0 %all-to-all-start = ((bf16[64,32,128]{2,1,0:T(8,128)(2,1)}), bf16[64,32,128]{2,1,0:T(8,128)(2,1)S(1)}, u32[]{:S(2)}, u32[]{:S(2)}) async-start(bf16[64,32,128]{2,1,0:T(8,128)(2,1)} %broadcast_in_dim.3), calls=%async_computation | async-start | bytes 1048576 | tf_op jit(solution)/shard_map/all_to_all | solution.py:281
  23.5 6.0 %collective-permute-start = (s32[2]{0:T(128)S(1)}, s32[2]{0:T(128)S(1)}, u32[]{:S(2)}, u32[]{:S(2)}) collective-permute-start(s32[2]{0:T(128)S(1)} %copy-done.2), channel_id=1, source_target_pairs={{0,1},{1,0},{2,3},{3,2},{4,5},{5,4},{6,7},{7,6},{8,9},{9,8},{10,11... | collective-permute-start | bytes 32 | tf_op jit(solution)/shard_map/ppermute | solution.py:282
  37.1 6.5 %copy-start = (bf16[2,1024]{1,0:T(2,128)(2,1)S(1)}, bf16[2,1024]{1,0:T(2,128)(2,1)}, u32[]{:S(2)}) copy-start(bf16[2,1024]{1,0:T(2,128)(2,1)} %queries_ref.1) | copy-start | bytes 12292
  37.1 8.6 %collective-permute-start.1 = (bf16[80,128]{1,0:T(8,128)(2,1)S(1)}, bf16[80,128]{1,0:T(8,128)(2,1)S(1)}, u32[]{:S(2)}, u32[]{:S(2)}) collective-permute-start(bf16[80,128]{1,0:T(8,128)(2,1)S(1)} %shard_map.46), channel_id=1, source_target_pairs={{0,1},{1,0},{2,3},{3,2},{4,5},{5,4},{6,7},{7,6},{8,9},{9,8},{10,11... | collective-permute-start | bytes 61448 | tf_op jit(solution)/shard_map/ppermute | solution.py:285
  43.7 0.7 %copy-start.1 = (s32[2]{0:T(128)S(1)}, s32[2]{0:T(128)}, u32[]{:S(2)}) copy-start(s32[2]{0:T(128)} %lengths_ref.1) | copy-start | bytes 28

commit v5 on v4

--- a/solution.py
+++ b/solution.py
@@ -78,6 +78,14 @@
         for b in range(rows):
             wide = jnp.broadcast_to(centre[b : b + 1], (LANES, LANES))
             centre_ref[s, LANES * b : LANES * (b + 1), :] = wide.T
+
+
+def spread(block_ref, out_ref, arrived):
+    copies = [pltpu.make_async_copy(block_ref, out_ref.at[p], arrived.at[p]) for p in range(out_ref.shape[0])]
+    for copy in copies:
+        copy.start()
+    for copy in copies:
+        copy.wait()
 
 
 def pick(theirs_ref, gathered_ref, out_ref):
@@ -278,7 +286,15 @@
     overall = chips * CORES * long_series.shape[0]
     swap = [(0, 1), (1, 0)]
     block = long_series.reshape(rows, LANES)
-    gathered = lax.all_to_all(jnp.broadcast_to(block, (chips, rows, LANES)), "chip", 0, 0, tiled=True)
+    copies = pl.pallas_call(
+        spread,
+        out_shape=jax.ShapeDtypeStruct((chips, rows, LANES), jnp.bfloat16),
+        in_specs=[pl.BlockSpec(memory_space=pltpu.HBM)],
+        out_specs=pl.BlockSpec(memory_space=pltpu.HBM),
+        scratch_shapes=[pltpu.SemaphoreType.DMA((chips,))],
+        name="spread",
+    )(block)
+    gathered = lax.all_to_all(copies, "chip", 0, 0, tiled=True)
     theirs = lax.ppermute(groups, "core", swap)
     windows, centre, ends = prepare_call(slots, query_len)(lengths, queries, queries[:, ::-1])
     picked = call(pick, jax.ShapeDtypeStruct(((rows + 8) * slots, LANES), jnp.bfloat16), [SMEM, VMEM])(theirs, gathered)

time: 54.3 us -> 70.1 us (1.29)
  Pallas kernels: 10.2 us -> 27.7 us
  local copies, waits for them, and re-layouts: 2.29 us -> 0.74 us
    pallas_call x0 -> x1, Pallas kernels: none -> 17.6 us  [body(): pl.pallas_call(spread, out_shape=jax.ShapeDtypeStruct((chips, rows, LANES...]
    broadcast_in_dim x1 -> x0, local copies, waits for them, and re-layouts: 1.55 us -> none  [body(): jnp.broadcast_to(block, (chips, rows, LANES))]
  transfers between devices with their start and end apart: 3 -> 3, of which waited for: 2 -> 2; matrix products, arithmetic and copies ran while one was open for 1% -> 1% of each run, Pallas kernels for 3% -> 2%
where the time goes in v5:
time: 70.1 us; the launch traced here: 69.9 us
  starting transfers between devices  33.6 us (48%)
  Pallas kernels  27.7 us (40%)
  waiting for transfers between devices  7.82 us (11%)
  local copies, waits for them, and re-layouts  0.74 us (1%)
    all_to_all x1, starting transfers between devices, body(): gathered = lax.all_to_all(copies, 'chip', 0, 0, tiled=True)  21.8 us
    pallas_call x1, Pallas kernels, body(): pl.pallas_call(spread, out_shape=jax.ShapeDtypeStruct((chips, rows, LANES...  17.6 us
    pallas_call x1, Pallas kernels, body(): join_call(slots, rows, query_len, overall)  8.21 us
    all_to_all x1, waiting for transfers between devices, body(): gathered = lax.all_to_all(copies, 'chip', 0, 0, tiled=True)  7 us
    ppermute x1, starting transfers between devices, body(): passed = lax.ppermute(picked, 'core', swap)  6.51 us
    ppermute x1, starting transfers between devices, body(): theirs = lax.ppermute(groups, 'core', swap)  5.23 us
  transfers between devices with their start and end apart: 3, of which 2 were waited for; matrix products, arithmetic and copies ran while one was open for 1% of the time, Pallas kernels for 2%

profile of v5, /device:TPU:513, one launch (start us, length us, event | category | flops | bytes accessed | tf_op | source)
XLA Modules:
  0.0 69.9 jit_solution(4574316328461987804)
XLA Ops:
  0.0 17.6 %spread.1 = bf16[64,32,128]{2,1,0:T(8,128)(2,1)} custom-call(bf16[32,128]{1,0:T(8,128)(2,1)} %bitcast.2), custom_call_target="tpu_custom_call" | custom-call | tf_op jit(solution)/shard_map/spread/pallas_call | solution.py:289
  17.6 0.0 copy-start.2
  17.6 21.8 %all-to-all-start = ((bf16[64,32,128]{2,1,0:T(8,128)(2,1)}), bf16[64,32,128]{2,1,0:T(8,128)(2,1)S(1)}, u32[]{:S(2)}, u32[]{:S(2)}) async-start(bf16[64,32,128]{2,1,0:T(8,128)(2,1)} %spread.1), calls=%async_computation | async-start | bytes 1048576 | tf_op jit(solution)/shard_map/all_to_all | solution.py:297
  39.4 0.0 copy-done.2
  39.4 5.2 %collective-permute-start = (s32[2]{0:T(128)S(1)}, s32[2]{0:T(128)S(1)}, u32[]{:S(2)}, u32[]{:S(2)}) collective-permute-start(s32[2]{0:T(128)S(1)} %copy-done.2), channel_id=1, source_target_pairs={{0,1},{1,0},{2,3},{3,2},{4,5},{5,4},{6,7},{7,6},{8,9},{9,8},{10,11... | collective-permute-start | bytes 32 | tf_op jit(solution)/shard_map/ppermute | solution.py:298
  44.6 0.8 %collective-permute-done.theirs_ref = s32[2]{0:T(128)S(1)} collective-permute-done((s32[2]{0:T(128)S(1)}, s32[2]{0:T(128)S(1)}, u32[]{:S(2)}, u32[]{:S(2)}) %collective-permute-start) | collective-permute-done | bytes 40 | tf_op jit(solution)/shard_map/ppermute | solution.py:298
  45.5 7.0 %all-to-all-done.gathered_ref = bf16[64,32,128]{2,1,0:T(8,128)(2,1)S(1)} async-done(((bf16[64,32,128]{2,1,0:T(8,128)(2,1)}), bf16[64,32,128]{2,1,0:T(8,128)(2,1)S(1)}, u32[]{:S(2)}, u32[]{:S(2)}) %all-to-all-start) | async-done | bytes 524320 | tf_op jit(solution)/shard_map/all_to_all | solution.py:297
  52.5 0.6 shard_map.46
  53.0 0.0 copy-start
  53.1 6.5 %collective-permute-start.1 = (bf16[80,128]{1,0:T(8,128)(2,1)S(1)}, bf16[80,128]{1,0:T(8,128)(2,1)S(1)}, u32[]{:S(2)}, u32[]{:S(2)}) collective-permute-start(bf16[80,128]{1,0:T(8,128)(2,1)S(1)} %shard_map.46), channel_id=1, source_target_pairs={{0,1},{1,0},{2,3},{3,2},{4,5},{5,4},{6,7},{7,6},{8,9},{9,8},{10,11... | collective-permute-start | bytes 61448 | tf_op jit(solution)/shard_map/ppermute | solution.py:301
  59.6 0.0 copy-done
  59.6 0.0 copy-start.1
  59.6 0.7 %rev.3.turned_ref = bf16[2,1024]{1,0:T(2,128)(2,1)S(1)} reverse(bf16[2,1024]{1,0:T(2,128)(2,1)S(1)} %copy-done), dimensions={1} | reverse | bytes 8192 | tf_op jit(solution)/shard_map/rev | solution.py:299
  60.3 0.0 copy-done.1
  60.3 1.4 %shard_map.47 = (bf16[2,1152,128]{2,1,0:T(8,128)(2,1)S(1)}, f32[2,1024,128]{2,1,0:T(8,128)S(1)}, f32[2,2,8,128]{3,2,1,0:T(8,128)S(1)}) custom-call(s32[2]{0:T(128)S(1)} %copy-done.1, bf16[2,1024]{1,0:T(2,128)(2,1)S(1)} %copy-done, bf16[2,1024]{1,0:T(2,128)(2,1)S(1)} %rev.3.turned_ref), custom_call_target="tpu_custom_call" | custom-call | tf_op jit(solution)/shard_map/pallas_call | solution.py:299
  61.7 0.0 collective-permute-done.1.passed_ref
  61.7 8.2 %shard_map.48 = f32[2,1024]{1,0:T(2,128)} custom-call(s32[1]{0:T(128)} %bitcast.core_ref, s32[2]{0:T(128)S(1)} %copy-done.2, bf16[64,32,128]{2,1,0:T(8,128)(2,1)S(1)} %all-to-all-done.gathered_ref, bf16[80,128]{1,0:T(8,128)(2,1)S(1)} %collective-permute-done.1.passed_ref, bf16[2,1152,128]{2,1,0:T(8,128)(2,1)S(1)} %get-tuple-element.8.windows_ref, ...), custom_call_target="tpu_custom_call" | custom-call | tf_op jit(solution)/shard_map/pallas_call | solution.py:303
Async XLA Ops:
  17.6 21.8 %copy-start.2 = (s32[2]{0:T(128)S(1)}, s32[2]{0:T(128)}, u32[]{:S(2)}) copy-start(s32[2]{0:T(128)} %groups_ref.1) | copy-start | bytes 28
  17.6 34.9 %all-to-all-start = ((bf16[64,32,128]{2,1,0:T(8,128)(2,1)}), bf16[64,32,128]{2,1,0:T(8,128)(2,1)S(1)}, u32[]{:S(2)}, u32[]{:S(2)}) async-start(bf16[64,32,128]{2,1,0:T(8,128)(2,1)} %spread.1), calls=%async_computation | async-start | bytes 1048576 | tf_op jit(solution)/shard_map/all_to_all | solution.py:297
  39.4 6.0 %collective-permute-start = (s32[2]{0:T(128)S(1)}, s32[2]{0:T(128)S(1)}, u32[]{:S(2)}, u32[]{:S(2)}) collective-permute-start(s32[2]{0:T(128)S(1)} %copy-done.2), channel_id=1, source_target_pairs={{0,1},{1,0},{2,3},{3,2},{4,5},{5,4},{6,7},{7,6},{8,9},{9,8},{10,11... | collective-permute-start | bytes 32 | tf_op jit(solution)/shard_map/ppermute | solution.py:298
  53.0 6.5 %copy-start = (bf16[2,1024]{1,0:T(2,128)(2,1)S(1)}, bf16[2,1024]{1,0:T(2,128)(2,1)}, u32[]{:S(2)}) copy-start(bf16[2,1024]{1,0:T(2,128)(2,1)} %queries_ref.1) | copy-start | bytes 12292
  53.1 8.6 %collective-permute-start.1 = (bf16[80,128]{1,0:T(8,128)(2,1)S(1)}, bf16[80,128]{1,0:T(8,128)(2,1)S(1)}, u32[]{:S(2)}, u32[]{:S(2)}) collective-permute-start(bf16[80,128]{1,0:T(8,128)(2,1)S(1)} %shard_map.46), channel_id=1, source_target_pairs={{0,1},{1,0},{2,3},{3,2},{4,5},{5,4},{6,7},{7,6},{8,9},{9,8},{10,11... | collective-permute-start | bytes 61448 | tf_op jit(solution)/shard_map/ppermute | solution.py:301
  59.6 0.7 %copy-start.1 = (s32[2]{0:T(128)S(1)}, s32[2]{0:T(128)}, u32[]{:S(2)}) copy-start(s32[2]{0:T(128)} %lengths_ref.1) | copy-start | bytes 28

commit v6 on v5

--- a/solution.py
+++ b/solution.py
@@ -80,8 +80,14 @@
             centre_ref[s, LANES * b : LANES * (b + 1), :] = wide.T
 
 
-def spread(block_ref, out_ref, arrived):
-    copies = [pltpu.make_async_copy(block_ref, out_ref.at[p], arrived.at[p]) for p in range(out_ref.shape[0])]
+def spread(block_ref, out_ref, several, left):
+    each = several.shape[0]
+    for k in range(each):
+        several[k] = block_ref[...]
+    copies = [
+        pltpu.make_async_copy(several, out_ref.at[pl.ds(each * p, each)], left.at[p])
+        for p in range(out_ref.shape[0] // each)
+    ]
     for copy in copies:
         copy.start()
     for copy in copies:
@@ -289,9 +295,9 @@
     copies = pl.pallas_call(
         spread,
         out_shape=jax.ShapeDtypeStruct((chips, rows, LANES), jnp.bfloat16),
-        in_specs=[pl.BlockSpec(memory_space=pltpu.HBM)],
+        in_specs=[VMEM],
         out_specs=pl.BlockSpec(memory_space=pltpu.HBM),
-        scratch_shapes=[pltpu.SemaphoreType.DMA((chips,))],
+        scratch_shapes=[pltpu.VMEM((8, rows, LANES), jnp.bfloat16), pltpu.SemaphoreType.DMA((chips // 8,))],
         name="spread",
     )(block)
     gathered = lax.all_to_all(copies, "chip", 0, 0, tiled=True)

time: 70.1 us -> 54.2 us (0.77)
  Pallas kernels: 27.7 us -> 11.7 us
    pallas_call x1, Pallas kernels: 17.6 us -> 1.56 us  [body(): pl.pallas_call(spread, out_shape=jax.ShapeDtypeStruct((chips, rows, LANES...]
  transfers between devices with their start and end apart: 3 -> 3, of which waited for: 2 -> 2; matrix products, arithmetic and copies ran while one was open for 1% -> 1% of each run, Pallas kernels for 2% -> 3%
where the time goes in v6:
time: 54.2 us; the launch traced here: 53.9 us
  starting transfers between devices  33.6 us (62%)
  Pallas kernels  11.7 us (22%)
  waiting for transfers between devices  7.82 us (14%)
  local copies, waits for them, and re-layouts  0.74 us (1%)
    all_to_all x1, starting transfers between devices, body(): gathered = lax.all_to_all(copies, 'chip', 0, 0, tiled=True)  21.8 us
    pallas_call x1, Pallas kernels, body(): join_call(slots, rows, query_len, overall)  8.21 us
    all_to_all x1, waiting for transfers between devices, body(): gathered = lax.all_to_all(copies, 'chip', 0, 0, tiled=True)  7 us
    ppermute x1, starting transfers between devices, body(): passed = lax.ppermute(picked, 'core', swap)  6.51 us
    ppermute x1, starting transfers between devices, body(): theirs = lax.ppermute(groups, 'core', swap)  5.23 us
    pallas_call x1, Pallas kernels, body(): pl.pallas_call(spread, out_shape=jax.ShapeDtypeStruct((chips, rows, LANES...  1.56 us
    pallas_call x1, Pallas kernels, body(): prepare_call(slots, query_len)(lengths, queries, queries[:, ::-1])  1.38 us
  transfers between devices with their start and end apart: 3, of which 2 were waited for; matrix products, arithmetic and copies ran while one was open for 1% of the time, Pallas kernels for 3%

profile of v6, /device:TPU:513, one launch (start us, length us, event | category | flops | bytes accessed | tf_op | source)
XLA Modules:
  0.0 53.9 jit_solution(10535037346192305337)
XLA Ops:
  0.0 1.6 %spread.1 = bf16[64,32,128]{2,1,0:T(8,128)(2,1)} custom-call(bf16[32,128]{1,0:T(8,128)(2,1)} %bitcast.2), custom_call_target="tpu_custom_call" | custom-call | tf_op jit(solution)/shard_map/spread/pallas_call | solution.py:295
  1.6 0.0 copy-start.2
  1.6 21.8 %all-to-all-start = ((bf16[64,32,128]{2,1,0:T(8,128)(2,1)}), bf16[64,32,128]{2,1,0:T(8,128)(2,1)S(1)}, u32[]{:S(2)}, u32[]{:S(2)}) async-start(bf16[64,32,128]{2,1,0:T(8,128)(2,1)} %spread.1), calls=%async_computation | async-start | bytes 1048576 | tf_op jit(solution)/shard_map/all_to_all | solution.py:303
  23.4 0.0 copy-done.2
  23.4 5.2 %collective-permute-start = (s32[2]{0:T(128)S(1)}, s32[2]{0:T(128)S(1)}, u32[]{:S(2)}, u32[]{:S(2)}) collective-permute-start(s32[2]{0:T(128)S(1)} %copy-done.2), channel_id=1, source_target_pairs={{0,1},{1,0},{2,3},{3,2},{4,5},{5,4},{6,7},{7,6},{8,9},{9,8},{10,11... | collective-permute-start | bytes 32 | tf_op jit(solution)/shard_map/ppermute | solution.py:304
  28.6 0.8 %collective-permute-done.theirs_ref = s32[2]{0:T(128)S(1)} collective-permute-done((s32[2]{0:T(128)S(1)}, s32[2]{0:T(128)S(1)}, u32[]{:S(2)}, u32[]{:S(2)}) %collective-permute-start) | collective-permute-done | bytes 40 | tf_op jit(solution)/shard_map/ppermute | solution.py:304
  29.5 7.0 %all-to-all-done.gathered_ref = bf16[64,32,128]{2,1,0:T(8,128)(2,1)S(1)} async-done(((bf16[64,32,128]{2,1,0:T(8,128)(2,1)}), bf16[64,32,128]{2,1,0:T(8,128)(2,1)S(1)}, u32[]{:S(2)}, u32[]{:S(2)}) %all-to-all-start) | async-done | bytes 524320 | tf_op jit(solution)/shard_map/all_to_all | solution.py:303
  36.5 0.6 %shard_map.46 = bf16[80,128]{1,0:T(8,128)(2,1)S(1)} custom-call(s32[2]{0:T(128)S(1)} %collective-permute-done.theirs_ref, bf16[64,32,128]{2,1,0:T(8,128)(2,1)S(1)} %all-to-all-done.gathered_ref), custom_call_target="tpu_custom_call" | custom-call | tf_op jit(solution)/shard_map/pallas_call | solution.py:306
  37.0 0.0 copy-start
  37.0 6.5 %collective-permute-start.1 = (bf16[80,128]{1,0:T(8,128)(2,1)S(1)}, bf16[80,128]{1,0:T(8,128)(2,1)S(1)}, u32[]{:S(2)}, u32[]{:S(2)}) collective-permute-start(bf16[80,128]{1,0:T(8,128)(2,1)S(1)} %shard_map.46), channel_id=1, source_target_pairs={{0,1},{1,0},{2,3},{3,2},{4,5},{5,4},{6,7},{7,6},{8,9},{9,8},{10,11... | collective-permute-start | bytes 61448 | tf_op jit(solution)/shard_map/ppermute | solution.py:307
  43.6 0.0 copy-done
  43.6 0.0 copy-start.1
  43.6 0.7 %rev.3.turned_ref = bf16[2,1024]{1,0:T(2,128)(2,1)S(1)} reverse(bf16[2,1024]{1,0:T(2,128)(2,1)S(1)} %copy-done), dimensions={1} | reverse | bytes 8192 | tf_op jit(solution)/shard_map/rev | solution.py:305
  44.3 0.0 copy-done.1
  44.3 1.4 %shard_map.47 = (bf16[2,1152,128]{2,1,0:T(8,128)(2,1)S(1)}, f32[2,1024,128]{2,1,0:T(8,128)S(1)}, f32[2,2,8,128]{3,2,1,0:T(8,128)S(1)}) custom-call(s32[2]{0:T(128)S(1)} %copy-done.1, bf16[2,1024]{1,0:T(2,128)(2,1)S(1)} %copy-done, bf16[2,1024]{1,0:T(2,128)(2,1)S(1)} %rev.3.turned_ref), custom_call_target="tpu_custom_call" | custom-call | tf_op jit(solution)/shard_map/pallas_call | solution.py:305
  45.7 0.0 collective-permute-done.1.passed_ref
  45.7 8.2 %shard_map.48 = f32[2,1024]{1,0:T(2,128)} custom-call(s32[1]{0:T(128)} %bitcast.core_ref, s32[2]{0:T(128)S(1)} %copy-done.2, bf16[64,32,128]{2,1,0:T(8,128)(2,1)S(1)} %all-to-all-done.gathered_ref, bf16[80,128]{1,0:T(8,128)(2,1)S(1)} %collective-permute-done.1.passed_ref, bf16[2,1152,128]{2,1,0:T(8,128)(2,1)S(1)} %get-tuple-element.8.windows_ref, ...), custom_call_target="tpu_custom_call" | custom-call | tf_op jit(solution)/shard_map/pallas_call | solution.py:309
Async XLA Ops:
  1.6 21.8 %copy-start.2 = (s32[2]{0:T(128)S(1)}, s32[2]{0:T(128)}, u32[]{:S(2)}) copy-start(s32[2]{0:T(128)} %groups_ref.1) | copy-start | bytes 28
  1.6 34.9 %all-to-all-start = ((bf16[64,32,128]{2,1,0:T(8,128)(2,1)}), bf16[64,32,128]{2,1,0:T(8,128)(2,1)S(1)}, u32[]{:S(2)}, u32[]{:S(2)}) async-start(bf16[64,32,128]{2,1,0:T(8,128)(2,1)} %spread.1), calls=%async_computation | async-start | bytes 1048576 | tf_op jit(solution)/shard_map/all_to_all | solution.py:303
  23.4 6.0 %collective-permute-start = (s32[2]{0:T(128)S(1)}, s32[2]{0:T(128)S(1)}, u32[]{:S(2)}, u32[]{:S(2)}) collective-permute-start(s32[2]{0:T(128)S(1)} %copy-done.2), channel_id=1, source_target_pairs={{0,1},{1,0},{2,3},{3,2},{4,5},{5,4},{6,7},{7,6},{8,9},{9,8},{10,11... | collective-permute-start | bytes 32 | tf_op jit(solution)/shard_map/ppermute | solution.py:304
  37.0 6.5 %copy-start = (bf16[2,1024]{1,0:T(2,128)(2,1)S(1)}, bf16[2,1024]{1,0:T(2,128)(2,1)}, u32[]{:S(2)}) copy-start(bf16[2,1024]{1,0:T(2,128)(2,1)} %queries_ref.1) | copy-start | bytes 12292
  37.0 8.6 %collective-permute-start.1 = (bf16[80,128]{1,0:T(8,128)(2,1)S(1)}, bf16[80,128]{1,0:T(8,128)(2,1)S(1)}, u32[]{:S(2)}, u32[]{:S(2)}) collective-permute-start(bf16[80,128]{1,0:T(8,128)(2,1)S(1)} %shard_map.46), channel_id=1, source_target_pairs={{0,1},{1,0},{2,3},{3,2},{4,5},{5,4},{6,7},{7,6},{8,9},{9,8},{10,11... | collective-permute-start | bytes 61448 | tf_op jit(solution)/shard_map/ppermute | solution.py:307
  43.6 0.7 %copy-start.1 = (s32[2]{0:T(128)S(1)}, s32[2]{0:T(128)}, u32[]{:S(2)}) copy-start(s32[2]{0:T(128)} %lengths_ref.1) | copy-start | bytes 28
